TPU v7x, 512 devices: a whole 4x8x8 slice. The times are simulated.
512 devices in a mesh: row: 16 (over x_hi, y), col: 32 (over x_lo, z, core).
Axes of the slice: x: 4 (x_hi: 2, x_lo: 2; x = x_hi * 2 + x_lo), y: 8, z: 8, core: 2. Of those that a mesh axis runs over, the one named last changes fastest.
Arguments:
- fact_block: int32 [1572864, 1], P(('row', 'col')), may hold values from 0 to 511; in each aligned block of 3072 rows (0 to 3071, 3072 to 6143, ...) at most 12 rows name the same one
- fact_offset: int32 [1572864], P(('row', 'col')), may hold values from 0 to 2047
- fact_date: int32 [1572864], P(('row', 'col')), may hold values from 0 to 2555
- revenue: bfloat16 [1572864], P(('row', 'col')), may hold values from 0.5 to 4
- supplier_words: int32 [35328], P('col'), may hold values from 0 to 1073741823
- date_words: int32 [96], P('col'), may hold values from 0 to 1073741823
- candidates: int32 [1024], replicated, may hold values from 0 to 1048575
Outputs:
- supplier_revenue: float32 [1048576], P(('row', 'col'))
- candidate_revenue: float32 [1024], replicated
- candidate_total: float32 [], replicated
Inputs may be any that keep to these rules, and one draw needn't show every extreme that they name: `fact_block`: each device's rows name no owner block more than 12 times. `candidates`: ids may repeat.
All inputs are finite; a program needn't handle non-finite values.
Results may differ from a plain program's by a relative error of at most 0.0003.
Values sent between devices are 32-bit elements; how exact they have to be, the bound alone decides.
No kernel may reach another device: no remote copies, remote signals or barrier semaphores. Data moves between devices by JAX's collectives and lax.ppermute only.
A program may use at most 64 MiB of HBM per device.

v0:
```python
import jax
import jax.numpy as jnp
from jax import lax
from jax.sharding import Mesh
from jax.sharding import PartitionSpec as P

SUP_DEV = 2048
ROW = ("row_0", "row_1")
COL = ("col_0", "col_1", "col_2")
ROW_COL = ("row_0", "row_1", "col_0", "col_1", "col_2")


def copy_for_each(x, axis):
    copies = jnp.broadcast_to(x, (lax.axis_size(axis), *x.shape))
    return lax.all_to_all(copies, axis, split_axis=0, concat_axis=0, tiled=True)


def joined_along(parts, dim):
    lengths = list(parts.shape[1:])
    lengths[dim] *= parts.shape[0]
    return jnp.moveaxis(parts, 0, dim).reshape(lengths)


def gather_directly(x, axis, dim):
    parts = copy_for_each(x, axis)
    return joined_along(parts, dim)


def over_axes(x, axes):
    for axis in axes:
        x = lax.psum(x, axis)
    return x


def filtered_revenue(owner, fact_offset, fact_date, revenue, supplier_all, date_all):
    words_per_block = (SUP_DEV + 29) // 30
    word_index = owner * words_per_block + fact_offset // 30
    supplier_word = jnp.take(supplier_all, word_index)
    supplier_bit = jnp.bitwise_and(jnp.right_shift(supplier_word, fact_offset % 30), 1)
    date_slot = fact_date // 30
    positions = jnp.arange(date_all.shape[0], dtype=jnp.int32)
    date_word = jnp.sum(
        jnp.where(date_slot[:, None] == positions[None, :], date_all[None, :], 0), axis=1
    )
    date_bit = jnp.bitwise_and(jnp.right_shift(date_word, fact_date % 30), 1)
    return jnp.where(supplier_bit * date_bit == 1, revenue, jnp.zeros_like(revenue))


def per_device(fact_block, fact_offset, fact_date, revenue, supplier_words, date_words, candidates):
    devices = lax.axis_size(ROW) * lax.axis_size(COL)
    supplier_all, date_all = (
        gather_directly(supplier_words, COL, 0),
        gather_directly(date_words, COL, 0),
    )
    owner = fact_block[:, 0]
    masked = filtered_revenue(owner, fact_offset, fact_date, revenue, supplier_all, date_all)
    row_count = fact_offset.shape[0]
    capacity = max(2, 2 * row_count // devices)
    row_ids = jnp.arange(row_count, dtype=jnp.int32)
    earlier = (owner[:, None] == owner[None, :]) & (row_ids[None, :] < row_ids[:, None])
    ranking = jnp.sum(earlier, axis=1, dtype=jnp.int32)
    slot_index = owner * capacity + ranking
    slot_revenue = (
        jnp.zeros((devices * capacity,), jnp.float32).at[slot_index].set(masked.astype(jnp.float32))
    )
    slot_offset = (
        jnp.zeros((devices * capacity,), jnp.float32)
        .at[slot_index]
        .set(fact_offset.astype(jnp.float32))
    )
    payload = jnp.stack((slot_revenue, slot_offset), axis=-1)
    payload = payload.reshape(lax.axis_size(ROW), lax.axis_size(COL), 2 * capacity)
    arrived = lax.all_to_all(
        lax.all_to_all(payload, COL, split_axis=1, concat_axis=1, tiled=True),
        ROW,
        split_axis=0,
        concat_axis=0,
        tiled=True,
    )
    arrived = arrived.reshape(-1, 2)
    owned = jax.ops.segment_sum(
        arrived[:, 0], arrived[:, 1].astype(jnp.int32), num_segments=SUP_DEV
    )
    global_id = owner * SUP_DEV + fact_offset
    onehot_cands = (global_id[:, None] == candidates[None, :]).astype(jnp.bfloat16)
    own_terms = jnp.dot(masked[None, :], onehot_cands, preferred_element_type=jnp.float32)[0]
    candidate_revenue = over_axes(own_terms, ROW_COL)
    candidate_total = jnp.sum(candidate_revenue)
    return (owned, candidate_revenue, candidate_total)


def solution(mesh):
    split = Mesh(mesh.devices.reshape(2, 8, 2, 8, 2), ("row_0", "row_1", "col_0", "col_1", "col_2"))
    return jax.shard_map(
        per_device,
        mesh=split,
        in_specs=(P(ROW_COL, None), P(ROW_COL), P(ROW_COL), P(ROW_COL), P(COL), P(COL), P()),
        out_specs=(P(ROW_COL), P(), P()),
        check_vma=False,
    )
```

profile of v0, /device:TPU:1, one launch (start us, length us, event | category | flops | bytes accessed | tf_op | source)
XLA Modules:
  0.0 197.6 jit_solution(4576482019518081585)
XLA Ops:
  0.6 1.3 broadcast_in_dim.48
  1.9 12.9 %all-to-all-start.1 = ((s32[32,1,3]{2,1,0:T(1,128)}), s32[32,1,3]{2,1,0:T(1,128)S(1)}, u32[]{:S(2)}, u32[]{:S(2)}) async-start(s32[32,1,3]{2,1,0:T(1,128)} %broadcast_in_dim.48), calls=%async_computation.1 | async-start | bytes 32768 | tf_op jit(solution)/shard_map/all_to_all | solution.py:15
  14.8 3.9 %convert_reduce_fusion = s32[3072]{0:T(1024)S(1)} fusion(s32[3072]{0:T(1024)} %bitcast.19), kind=kLoop, calls=%fused_computation.4 | loop fusion | flops 47182848 | bytes 24576 | tf_op jit(solution)/shard_map/reduce_sum | solution.py:61
  18.6 0.7 compare_select_fusion
  19.4 0.8 multiply_add_fusion
  20.2 11.8 %scatter_custom_fusion.1 = f32[6144]{0:T(1024)S(1)} fusion(s32[3072]{0:T(1024)S(1)} %bitcast.24, f32[3072]{0:T(1024)S(1)} %get-tuple-element.7, f32[]{:T(128)} %constant.30.clone.1), kind=kCustom, calls=%fused_computation.33 | custom fusion | bytes 24580 | tf_op jit(solution)/shard_map/scatter | solution.py:69
  32.0 0.0 all-to-all-done.1
  32.0 1.4 broadcast_in_dim.45
  33.4 8.3 %all-to-all-start = ((s32[32,1,1104]{2,1,0:T(1,128)}), s32[32,1,1104]{2,1,0:T(1,128)S(1)}, u32[]{:S(2)}, u32[]{:S(2)}) async-start(s32[32,1,1104]{2,1,0:T(1,128)} %broadcast_in_dim.45), calls=%async_computation | async-start | bytes 294912 | tf_op jit(solution)/shard_map/all_to_all | solution.py:15
  41.8 0.7 add_select_fusion.1
  42.5 0.5 broadcast.67
  43.0 0.7 reduce.8
  43.7 0.1 broadcast_in_dim.49
  43.8 0.3 select_reduce_fusion
  44.1 7.0 %all-to-all-done = s32[32,1,1104]{2,1,0:T(1,128)S(1)} async-done(((s32[32,1,1104]{2,1,0:T(1,128)}), s32[32,1,1104]{2,1,0:T(1,128)S(1)}, u32[]{:S(2)}, u32[]{:S(2)}) %all-to-all-start) | async-done | bytes 141344 | tf_op jit(solution)/shard_map/all_to_all | solution.py:15
  51.1 0.3 reduce
  51.4 0.1 reshape.40
  51.5 0.0 copy-start
  51.6 0.0 copy-start.1
  51.6 0.0 copy-start.2
  51.6 0.0 copy-start.4
  51.6 17.4 %gather_fusion = s32[3072]{0:T(1024)S(1)} fusion(s32[35328]{0:T(1024)S(1)} %reshape.40, s32[3072]{0:T(1024)S(1)} %get-tuple-element.6), kind=kCustom, calls=%fused_computation | custom fusion | bytes 36864 | tf_op jit(solution)/shard_map/jit(_take)/gather | solution.py:38
  69.0 0.0 copy-done
  69.0 0.0 copy-done.1
  69.0 0.0 copy-done.2
  69.0 0.0 copy-done.4
  69.1 11.8 %scatter_custom_fusion = f32[6144]{0:T(1024)S(1)} fusion(s32[3072]{0:T(1024)S(1)} %bitcast.25, f32[3072]{0:T(1024)S(1)} %get-tuple-element.3, f32[]{:T(128)} %constant.30.clone.1), kind=kCustom, calls=%fused_computation.35 | custom fusion | bytes 24580 | tf_op jit(solution)/shard_map/scatter | solution.py:64
  81.0 1.1 copy.15
  82.0 0.0 copy-start.5
  82.0 0.8 reshape.41
  82.9 0.2 copy.20
  83.0 0.8 reshape.96
  83.9 5.2 %all-to-all-start.2 = ((f32[32,1,384]{2,1,0:T(1,128)}), f32[32,1,384]{2,1,0:T(1,128)S(1)}, u32[]{:S(2)}, u32[]{:S(2)}) async-start(f32[32,1,384]{2,1,0:T(1,128)} %reshape.96), calls=%async_computation.2 | async-start | bytes 98304 | tf_op jit(solution)/shard_map/all_to_all | solution.py:74
  89.1 8.1 %all-to-all-done.2 = f32[32,1,384]{2,1,0:T(1,128)S(1)} async-done(((f32[32,1,384]{2,1,0:T(1,128)}), f32[32,1,384]{2,1,0:T(1,128)S(1)}, u32[]{:S(2)}, u32[]{:S(2)}) %all-to-all-start.2) | async-done | bytes 49184 | tf_op jit(solution)/shard_map/all_to_all | solution.py:74
  97.2 0.5 broadcast.70
  97.7 0.8 reduce.9
  98.4 0.2 reshape.97
  98.6 0.2 copy.17
  98.8 0.8 reshape.98
  99.5 9.1 %all-to-all-start.3 = ((f32[16,1,768]{2,1,0:T(1,128)}), f32[16,1,768]{2,1,0:T(1,128)S(1)}, u32[]{:S(2)}, u32[]{:S(2)}) async-start(f32[16,1,768]{2,1,0:T(1,128)} %reshape.98), calls=%async_computation.3 | async-start | bytes 98304 | tf_op jit(solution)/shard_map/all_to_all | solution.py:73
  108.7 0.0 copy-done.5
  108.7 2.0 %fusion.1 = f32[1,1024]{1,0:T(1,128)S(1)} fusion(bf16[3072,1]{0,1:T(2,128)(2,1)S(1)} %reshape.76, s32[1024]{0:T(1024)S(1)} %copy-done.5, s32[3072]{0:T(1024)S(1)} %get-tuple-element.5), kind=kOutput, calls=%fused_computation.7 | convolution fusion | flops 9437184 | bytes 26624 | tf_op jit(solution)/shard_map/dot_general | solution.py:86
  110.7 5.6 %psum.35 = f32[1024]{0:T(1024)S(1)} all-reduce(f32[1024]{0:T(1024)S(1)} %bitcast.27), channel_id=1, replica_groups=mesh['row_0'=2,'row_1'=8,'col_0'=2,'col_1'=8,'col_2'=2] {'row_0'}, use_global_device_ids=true, to_apply=%region_5.6 | all-reduce | flops 1024 | bytes 8192 | tf_op jit(solution)/shard_map/psum | solution.py:31
  116.2 13.2 %psum.36 = f32[1024]{0:T(1024)S(1)} all-reduce(f32[1024]{0:T(1024)S(1)} %psum.35), channel_id=1, replica_groups=mesh['row_0'=2,'row_1'=8,'col_0'=2,'col_1'=8,'col_2'=2] {'row_1'}, use_global_device_ids=true, to_apply=%region_6.7 | all-reduce | flops 1024 | bytes 8192 | tf_op jit(solution)/shard_map/psum | solution.py:31
  129.4 3.8 %psum.37 = f32[1024]{0:T(1024)S(1)} all-reduce(f32[1024]{0:T(1024)S(1)} %psum.36), channel_id=1, replica_groups=mesh['row_0'=2,'row_1'=8,'col_0'=2,'col_1'=8,'col_2'=2] {'col_0'}, use_global_device_ids=true, to_apply=%region_7.8 | all-reduce | flops 1024 | bytes 8192 | tf_op jit(solution)/shard_map/psum | solution.py:31
  133.2 11.3 %psum.38 = f32[1024]{0:T(1024)S(1)} all-reduce(f32[1024]{0:T(1024)S(1)} %psum.37), channel_id=1, replica_groups=mesh['row_0'=2,'row_1'=8,'col_0'=2,'col_1'=8,'col_2'=2] {'col_1'}, use_global_device_ids=true, to_apply=%region_8.9 | all-reduce | flops 1024 | bytes 8192 | tf_op jit(solution)/shard_map/psum | solution.py:31
  144.5 12.9 %psum.39 = f32[1024]{0:T(1024)S(1)} all-reduce(f32[1024]{0:T(1024)S(1)} %psum.38), channel_id=1, replica_groups=mesh['row_0'=2,'row_1'=8,'col_0'=2,'col_1'=8,'col_2'=2] {'col_2'}, use_global_device_ids=true, to_apply=%region_9.10 | all-reduce | flops 1024 | bytes 8192 | tf_op jit(solution)/shard_map/psum | solution.py:31
  157.4 0.0 copy-start.3
  157.4 0.6 reduce_sum.32
  158.0 0.0 all-to-all-done.3
  158.0 0.8 reduce.10
  158.8 0.1 reshape.99
  158.9 0.1 copy.18
  159.0 0.8 reshape.42
  159.9 0.9 slice_reduce_fusion
  160.8 0.0 copy-done.3
  160.8 1.7 fusion.5
  162.5 35.1 %scatter_custom_fusion.2 = f32[2048]{0:T(1024)} fusion(s32[6144]{0:T(1024)S(1)} %fusion.5, f32[6144]{0:T(1024)S(1)} %slice_reduce_fusion, f32[]{:T(128)} %constant.30.clone.1), kind=kCustom, calls=%fused_computation.43 | custom fusion | flops 6144 | bytes 8196 | tf_op jit(solution)/shard_map/scatter-add | solution.py:81
  (3 shorter events, 0.1 us)
Async XLA Ops:
  1.9 30.1 %all-to-all-start.1 = ((s32[32,1,3]{2,1,0:T(1,128)}), s32[32,1,3]{2,1,0:T(1,128)S(1)}, u32[]{:S(2)}, u32[]{:S(2)}) async-start(s32[32,1,3]{2,1,0:T(1,128)} %broadcast_in_dim.48), calls=%async_computation.1 | async-start | bytes 32768 | tf_op jit(solution)/shard_map/all_to_all | solution.py:15
  33.4 17.6 %all-to-all-start = ((s32[32,1,1104]{2,1,0:T(1,128)}), s32[32,1,1104]{2,1,0:T(1,128)S(1)}, u32[]{:S(2)}, u32[]{:S(2)}) async-start(s32[32,1,1104]{2,1,0:T(1,128)} %broadcast_in_dim.45), calls=%async_computation | async-start | bytes 294912 | tf_op jit(solution)/shard_map/all_to_all | solution.py:15
  51.5 17.5 %copy-start = (s32[3072,1]{0,1:T(1,128)S(1)}, s32[3072,1]{0,1:T(1,128)}, u32[]{:S(2)}) copy-start(s32[3072,1]{0,1:T(1,128)} %param.7) | copy-start | bytes 36868
  51.6 17.5 %copy-start.1 = (s32[3072]{0:T(1024)S(1)}, s32[3072]{0:T(1024)}, u32[]{:S(2)}) copy-start(s32[3072]{0:T(1024)} %param.9) | copy-start | bytes 36868
  51.6 17.5 %copy-start.2 = (s32[3072]{0:T(1024)S(1)}, s32[3072]{0:T(1024)}, u32[]{:S(2)}) copy-start(s32[3072]{0:T(1024)} %param.8) | copy-start | bytes 36868
  51.6 17.5 %copy-start.4 = (bf16[3072]{0:T(1024)(128)(2,1)S(1)}, bf16[3072]{0:T(1024)(128)(2,1)}, u32[]{:S(2)}) copy-start(bf16[3072]{0:T(1024)(128)(2,1)} %param.10) | copy-start | bytes 18436
  82.0 26.6 %copy-start.5 = (s32[1024]{0:T(1024)S(1)}, s32[1024]{0:T(1024)}, u32[]{:S(2)}) copy-start(s32[1024]{0:T(1024)} %param.13) | copy-start | bytes 12292
  83.9 13.3 %all-to-all-start.2 = ((f32[32,1,384]{2,1,0:T(1,128)}), f32[32,1,384]{2,1,0:T(1,128)S(1)}, u32[]{:S(2)}, u32[]{:S(2)}) async-start(f32[32,1,384]{2,1,0:T(1,128)} %reshape.96), calls=%async_computation.2 | async-start | bytes 98304 | tf_op jit(solution)/shard_map/all_to_all | solution.py:74
  99.5 58.5 %all-to-all-start.3 = ((f32[16,1,768]{2,1,0:T(1,128)}), f32[16,1,768]{2,1,0:T(1,128)S(1)}, u32[]{:S(2)}, u32[]{:S(2)}) async-start(f32[16,1,768]{2,1,0:T(1,128)} %reshape.98), calls=%async_computation.3 | async-start | bytes 98304 | tf_op jit(solution)/shard_map/all_to_all | solution.py:73
  157.4 3.4 %copy-start.3 = (f32[1024]{0:T(1024)}, f32[1024]{0:T(1024)S(1)}, u32[]{:S(2)}) copy-start(f32[1024]{0:T(1024)S(1)} %psum.39) | copy-start | bytes 12292
where the time goes:
time: 200 us; the launch traced here: 198 us
  local copies, waits for them, and re-layouts  50.9 us (25%)
  blocking collectives  46.8 us (23%)
  other arithmetic  46.4 us (23%)
  starting transfers between devices  35.5 us (18%)
  waiting for transfers between devices  15.1 us (8%)
  matrix products  2.01 us (1%)
    psum x5, blocking collectives, over_axes(): x = lax.psum(x, axis)  46.8 us
    scatter-add x1, other arithmetic, per_device(): jax.ops.segment_sum(arrived[:, 0], arrived[:, 1].astype(jnp.int32), num_s...  35.1 us
    all_to_all x2, starting transfers between devices, copy_for_each(): return lax.all_to_all(copies, axis, split_axis=0, concat_axis=0, tiled=True)  21.2 us
    gather x1, local copies, waits for them, and re-layouts, filtered_revenue(): supplier_word = jnp.take(supplier_all, word_index)  17.4 us
    scatter x1, local copies, waits for them, and re-layouts, per_device(): slot_offset = jnp.zeros((devices * capacity,), jnp.float32).at[slot_index...  11.8 us
    scatter x1, local copies, waits for them, and re-layouts, per_device(): jnp.zeros((devices * capacity,), jnp.float32).at[slot_index]  11.8 us
    all_to_all x1, starting transfers between devices, per_device(): lax.all_to_all(lax.all_to_all(payload, COL, split_axis=1, concat_axis=1,...  9.1 us
    all_to_all x1, waiting for transfers between devices, per_device(): lax.all_to_all(payload, COL, split_axis=1, concat_axis=1, tiled=True)  8.08 us
  transfers between devices with their start and end apart: 4, of which 2 were waited for; matrix products, arithmetic and copies ran while one was open for 11% of the time, Pallas kernels for 0%

commit v1 on v0

v1 whole, which is shorter than its diff:
```python
import functools

import jax
import jax.numpy as jnp
from jax import lax
from jax.experimental import pallas as pl
from jax.experimental.pallas import tpu as pltpu
from jax.sharding import Mesh
from jax.sharding import PartitionSpec as P

ROW = ("row_0", "row_1")
COL = ("col_0", "col_1", "col_2")
ROW_COL = ROW + COL

NROW, NCOL, NDEV = 16, 32, 512
SUP_DEV = 2048
WORDS = 69
LANES = 128
CH = 24
F32, BF16, I32 = jnp.float32, jnp.bfloat16, jnp.int32
BITS_AT, DATES_AT = 72, 104


def iota(shape, dim):
    return lax.broadcasted_iota(I32, shape, dim)


def div30(x):
    return jnp.right_shift(x * 2185, 16)


def lane_gather(row, idx):
    table = jnp.broadcast_to(row, idx.shape)
    return jnp.take_along_axis(table, idx, axis=1, mode="promise_in_bounds")


def roll(x, shift):
    shift = shift % LANES
    return pltpu.roll(x, shift, 1) if shift else x


def lookup(words, idx):
    which, lane = jnp.right_shift(idx, 7), jnp.bitwise_and(idx, 127)
    out = lane_gather(words[0], lane)
    for i in range(1, len(words)):
        out = jnp.where(which == i, lane_gather(words[i], lane), out)
    return out


def k0_body(pos_ref, words_ref, dates_ref, cands_ref, out_ref):
    col = pos_ref[0]
    words = [words_ref[i : i + 1, :] for i in range(9)]
    cands = cands_ref[...]
    off = jnp.bitwise_and(cands, SUP_DEV - 1)
    block = jnp.right_shift(cands, 11) - 16 * col
    mine = (block >= 0) & (block < 16)
    slot = div30(off)
    word = lookup(words, jnp.where(mine, block * WORDS + slot, 0))
    bits = jnp.where(mine, jnp.bitwise_and(jnp.right_shift(word, off - 30 * slot), 1), 0)
    sub, lane = iota((8, LANES), 0), iota((8, LANES), 1)
    dates = jnp.broadcast_to(dates_ref[...], (8, LANES))
    for j in range(4):
        m = jnp.bitwise_and(4 * sub + j, 15)
        own = lookup(words, jnp.where(lane < WORDS, m * WORDS + lane, 0))
        row = jnp.where(lane < WORDS, own, 0)
        in_bits = (lane >= BITS_AT) & (lane < BITS_AT + 32)
        row = jnp.where(in_bits, roll(bits, BITS_AT - 32 * j), row)
        row = jnp.where((lane >= DATES_AT) & (lane < DATES_AT + 3), roll(dates, DATES_AT), row)
        out_ref[pl.ds(j, 8, stride=4), :] = row


def k1_body(block_ref, off_ref, date_ref, rev_ref, cands_ref, tab_ref, cand_ref, hot_ref, val_ref):
    block, off, date = block_ref[...], off_ref[...], date_ref[...]
    rev = rev_ref[...].astype(F32)

    def key_of(b):
        return (
            jnp.bitwise_and(jnp.right_shift(b, 5), 1) * 256
            + jnp.bitwise_and(b, 31) * 8
            + jnp.right_shift(b, 6)
        )

    key = key_of(block)
    own = iota((NDEV, LANES), 0)
    for i in range(CH):
        hot = jnp.where(own == key[i : i + 1, :], 1.0, 0.0).astype(BF16)
        hot_ref[:, i * LANES : (i + 1) * LANES] = hot
    nt = (((1,), (1,)), ((), ()))
    nn = (((1,), (0,)), ((), ()))
    dot = functools.partial(lax.dot_general, preferred_element_type=F32)
    chunk = jnp.where(
        jnp.right_shift(iota((32, CH * LANES), 1), 7) == iota((32, CH * LANES), 0), 1.0, 0.0
    ).astype(BF16)
    count = dot(chunk, hot_ref[...], nt)
    before = jnp.where(iota((32, 32), 1) < iota((32, 32), 0), 1.0, 0.0).astype(BF16)
    prefix = dot(before, count.astype(BF16), nn)
    base = dot(prefix.astype(BF16), hot_ref[...], nn)
    keys_down = jnp.transpose(jnp.concatenate([key, jnp.zeros((LANES - CH, LANES), I32)], 0))
    earlier = iota((LANES, LANES), 0) < iota((LANES, LANES), 1)
    off_hi = jnp.right_shift(off, 7)
    off_lo = jnp.bitwise_and(off, 127)
    date_q = div30(date)
    date_r = date - 30 * date_q
    date_c = jnp.right_shift(date_q * 43691, 17)
    date_l = date_c + 32 * (date_q - 3 * date_c)
    values = [off_lo.astype(F32), off_hi.astype(F32), rev, date_l.astype(F32), date_r.astype(F32)]
    slots = iota((16, LANES), 0)
    for i in range(CH):
        same = (keys_down[:, i : i + 1] == key[i : i + 1, :]) & earlier
        inside = jnp.sum(jnp.where(same, 1.0, 0.0), axis=0, keepdims=True)
        rank = inside + base[i : i + 1, i * LANES : (i + 1) * LANES]
        here = slots == rank.astype(I32)
        for g, v in enumerate(values):
            val_ref[16 * g : 16 * g + 16, i * LANES : (i + 1) * LANES] = jnp.where(
                here, v[i : i + 1, :], 0.0
            ).astype(BF16)
    table = dot(val_ref[...], hot_ref[...], nt)
    tab_ref[0:16, :] = table[0:16] + 128.0 * table[16:32]
    tab_ref[16:64, :] = table[32:80]
    cands = cands_ref[...]
    cand_key = key_of(jnp.right_shift(cands, 11))
    cand_hot = jnp.where(iota((NDEV, 1024), 0) == cand_key, 1.0, 0.0).astype(BF16)
    named = dot(table.astype(BF16), cand_hot, nn)
    cand_off = jnp.bitwise_and(cands, SUP_DEV - 1).astype(F32)
    same_off = named[0:16] + 128.0 * named[16:32] == cand_off
    cand_ref[0:16, :] = jnp.where(same_off, named[32:48], 0.0)
    cand_ref[16:48, :] = named[48:80]


def k2_body(got_ref, tab_ref, cand_ref, out_ref, tmp_ref):
    got = got_ref[...]
    src, lane = iota((NCOL, LANES), 0), iota((NCOL, LANES), 1)
    table = jnp.zeros((NCOL, LANES), I32)
    for j in range(3):
        word = jnp.broadcast_to(got[:, DATES_AT + j : DATES_AT + j + 1], (NCOL, LANES))
        table = jnp.where(lane == 32 * j + src, word, table)
    table = jnp.sum(table, axis=0, keepdims=True)
    bits = jnp.sum(got, axis=0, keepdims=True)
    bits = roll(jnp.broadcast_to(bits, (8, LANES)), 64 - BITS_AT).astype(F32)
    lane8 = iota((8, LANES), 1)
    bits = jnp.where((iota((8, LANES), 0) == 0) & (lane8 >= 64) & (lane8 < 96), bits, 0.0)

    def date_ok(where, place):
        return jnp.bitwise_and(jnp.right_shift(lane_gather(table, where.astype(I32)), place.astype(I32)), 1) == 1

    for i in range(8):
        at = slice(i * LANES, (i + 1) * LANES)
        keep = date_ok(cand_ref[16:32, at], cand_ref[32:48, at])
        tmp_ref[i : i + 1, :] = jnp.sum(jnp.where(keep, cand_ref[0:16, at], 0.0), axis=0, keepdims=True)
    part = tmp_ref[...]
    kept = []
    for i in range(4):
        at = slice(i * LANES, (i + 1) * LANES)
        keep = date_ok(tab_ref[32:48, at], tab_ref[48:64, at])
        kept.append(jnp.where(keep, tab_ref[16:32, at], 0.0))
    for h in range(2):
        at, also = slice(h * LANES, (h + 1) * LANES), slice((h + 2) * LANES, (h + 3) * LANES)
        stack = jnp.concatenate(
            [tab_ref[0:16, at], kept[h], tab_ref[0:16, also], kept[h + 2], jnp.zeros((64, LANES), F32)], 0
        )
        tiles = jnp.transpose(stack)
        for t in range(16):
            out_ref[16 * h + t, 0:8, :] = tiles[8 * t : 8 * t + 8] + bits
            out_ref[16 * h + t, 8:16, :] = part


def k3_body(got_ref, out_ref):
    lane = iota((8, LANES), 1)
    bits = jnp.zeros((8, LANES), F32)
    for j in range(4):
        rows = roll(got_ref[pl.ds(16 * j, 8, stride=64), :], 32 * j - 64)
        bits = jnp.where(jnp.right_shift(lane, 5) == j, rows, bits)
    total = got_ref[8:16, :]
    for c in range(1, NCOL):
        total = total + got_ref[16 * c + 8 : 16 * c + 16, :]
    total = total * bits
    for hi in range(8):
        rows = got_ref[pl.ds(hi, NCOL, stride=16), :]
        for lo in range(2):
            tile = roll(rows[0:8], -32 * lo)
            for q in range(1, 4):
                tile = jnp.where(jnp.right_shift(lane, 5) == q, roll(rows[8 * q : 8 * q + 8], 32 * (q - lo)), tile)
            out_ref[2 * hi + lo, 0:8, :] = tile
            out_ref[2 * hi + lo, 8:16, :] = total


def k4_body(pos_ref, got_ref, words_ref, owned_ref, cand_ref, total_ref, hi_ref, lo_ref):
    lane = iota((8, LANES), 1)
    first = jnp.bitwise_and(lane, 16) == 0
    high, low = iota((16, LANES), 0), iota((LANES, LANES), 0)
    for p in range(8):
        even, odd = got_ref[2 * p, 0:8, :], got_ref[2 * p + 1, 0:8, :]
        off = jnp.where(first, even, roll(odd, 16)).astype(I32)
        rev = jnp.where(first, roll(even, -16), odd)
        off_hi, off_lo = jnp.right_shift(off, 7), jnp.bitwise_and(off, 127)
        for s in range(8):
            at = slice((8 * p + s) * LANES, (8 * p + s + 1) * LANES)
            hi_ref[:, at] = jnp.where(off_hi[s : s + 1] == high, rev[s : s + 1], 0.0).astype(BF16)
            lo_ref[:, at] = jnp.where(off_lo[s : s + 1] == low, 1.0, 0.0).astype(BF16)
    owned = lax.dot_general(
        hi_ref[...], lo_ref[...], (((1,), (1,)), ((), ())), preferred_element_type=F32
    )
    words = words_ref[pl.ds(2 * pos_ref[1] + jnp.right_shift(pos_ref[0], 4), 1), :]
    place = iota((16, LANES), 0) * LANES + iota((16, LANES), 1)
    slot = div30(place)
    bit = jnp.bitwise_and(jnp.right_shift(lane_gather(words, slot), place - 30 * slot), 1)
    owned_ref[...] = jnp.where(bit == 1, owned, 0.0)
    cand = got_ref[0, 8:16, :]
    for r in range(1, NROW):
        cand = cand + got_ref[r, 8:16, :]
    cand_ref[...] = cand
    total_ref[0, 0] = jnp.sum(cand)


SMEM = pl.BlockSpec(memory_space=pltpu.SMEM)
VMEM = pl.BlockSpec(memory_space=pltpu.VMEM)
shape = jax.ShapeDtypeStruct


def call(body, ins, outs, scratch=(), out_specs=None):
    return pl.pallas_call(
        body,
        out_shape=outs,
        in_specs=ins,
        out_specs=out_specs or (VMEM if not isinstance(outs, (tuple, list)) else [VMEM] * len(outs)),
        scratch_shapes=list(scratch),
        name=body.__name__,
    )


def per_device(fact_block, fact_offset, fact_date, revenue, supplier_words, date_words, candidates):
    pos = jnp.stack([lax.axis_index(COL), lax.axis_index(ROW)]).astype(I32)
    cands = candidates.reshape(8, LANES)
    words = jnp.pad(supplier_words, (0, 9 * LANES - 16 * WORDS)).reshape(9, LANES)
    dates = jnp.pad(date_words, (0, LANES - 3)).reshape(1, LANES)
    give0 = call(k0_body, [SMEM, VMEM, VMEM, VMEM], shape((NCOL, LANES), I32))(pos, words, dates, cands)
    got0 = lax.all_to_all(give0.reshape(NCOL, 1, LANES), COL, 0, 0, tiled=True).reshape(NCOL, LANES)
    tab, cand = call(
        k1_body,
        [VMEM] * 5,
        [shape((64, NDEV), F32), shape((48, 1024), F32)],
        [pltpu.VMEM((NDEV, CH * LANES), BF16), pltpu.VMEM((80, CH * LANES), BF16)],
    )(
        fact_block.reshape(CH, LANES),
        fact_offset.reshape(CH, LANES),
        fact_date.reshape(CH, LANES),
        revenue.reshape(CH, LANES),
        candidates.reshape(1, 1024),
    )
    give1 = call(k2_body, [VMEM] * 3, shape((NCOL, 16, LANES), F32), [pltpu.VMEM((8, LANES), F32)])(got0, tab, cand)
    got1 = lax.all_to_all(give1, COL, 0, 0, tiled=True)
    give2 = call(k3_body, [VMEM], shape((NROW, 16, LANES), F32))(got1.reshape(NCOL * 16, LANES))
    got2 = lax.all_to_all(give2, ROW, 0, 0, tiled=True)
    owned, cand, total = call(
        k4_body,
        [SMEM, VMEM, VMEM],
        [shape((16, LANES), F32), shape((8, LANES), F32), shape((1, 1), F32)],
        [pltpu.VMEM((16, 64 * LANES), BF16), pltpu.VMEM((LANES, 64 * LANES), BF16)],
        [VMEM, VMEM, SMEM],
    )(pos, got2, got0)
    return owned.reshape(SUP_DEV), cand.reshape(1024), total.reshape(())


def solution(mesh):
    split = Mesh(mesh.devices.reshape(2, 8, 2, 8, 2), ROW_COL)
    return jax.shard_map(
        per_device,
        mesh=split,
        in_specs=(P(ROW_COL, None), P(ROW_COL), P(ROW_COL), P(ROW_COL), P(COL), P(COL), P()),
        out_specs=(P(ROW_COL), P(), P()),
        check_vma=False,
    )
```

time: 200 us -> 69.2 us (0.35)
  the two profiles are of different devices: /device:TPU:1 before, /device:TPU:8 now
where the time goes in v1:
time: 69.2 us; the launch traced here: 68.7 us
  blocking collectives  37.2 us (54%)
  Pallas kernels  12.5 us (18%)
  starting transfers between devices  11.6 us (17%)
  waiting for transfers between devices  3.73 us (5%)
  local copies, waits for them, and re-layouts  2.37 us (3%)
    all_to_all x1, blocking collectives, per_device(): got2 = lax.all_to_all(give2, ROW, 0, 0, tiled=True)  19.3 us
    all_to_all x1, blocking collectives, per_device(): got1 = lax.all_to_all(give1, COL, 0, 0, tiled=True)  17.8 us
    all_to_all x1, starting transfers between devices, per_device(): lax.all_to_all(give0.reshape(NCOL, 1, LANES), COL, 0, 0, tiled=True)  11.6 us
    pallas_call x1, Pallas kernels, per_device(): call(k1_body, [VMEM] * 5, [shape((64, NDEV), F32), shape((48, 1024), F32)...  4.69 us
    all_to_all x1, waiting for transfers between devices, per_device(): lax.all_to_all(give0.reshape(NCOL, 1, LANES), COL, 0, 0, tiled=True)  3.73 us
    pallas_call x1, Pallas kernels, per_device(): call(k4_body, [SMEM, VMEM, VMEM], [shape((16, LANES), F32), shape((8, LAN...  2.53 us
    pallas_call x1, Pallas kernels, per_device(): call(k2_body, [VMEM] * 3, shape((NCOL, 16, LANES), F32), [pltpu.VMEM((8,...  2 us
    pallas_call x1, Pallas kernels, per_device(): call(k3_body, [VMEM], shape((NROW, 16, LANES), F32))  1.73 us
  transfers between devices with their start and end apart: 1, of which 1 were waited for; matrix products, arithmetic and copies ran while one was open for 0% of the time, Pallas kernels for 7%

profile of v1, /device:TPU:8, one launch (start us, length us, event | category | flops | bytes accessed | tf_op | source)
XLA Modules:
  0.0 68.7 jit_solution(4145897308353808378)
XLA Ops:
  0.6 0.0 copy-start.1
  0.7 0.0 copy-start.2
  0.7 0.6 copy-done.2
  1.3 0.5 pad_bitcast_fusion.1.dates_ref
  1.8 0.0 copy-done.1
  1.8 0.6 pad_bitcast_fusion.words_ref
  2.4 0.6 pad_add_fusion.pos_ref
  3.0 1.6 %k0_body.1 = s32[32,128]{1,0:T(8,128)} custom-call(s32[2]{0:T(128)} %pad_add_fusion.pos_ref, s32[9,128]{1,0:T(8,128)} %pad_bitcast_fusion.words_ref, s32[1,128]{1,0:T(1,128)} %pad_bitcast_fusion.1.dates_ref, s32[8,128]{1,0:T(8,128)} %bitcast.24), custom_call_target="tpu_custom_call" | custom-call | tf_op jit(solution)/shard_map/k0_body/pallas_call | solution.py:236
  4.6 11.6 %all-to-all-start = ((s32[32,1,128]{2,1,0:T(1,128)}), s32[32,1,128]{2,1,0:T(1,128)S(1)}, u32[]{:S(2)}, u32[]{:S(2)}) async-start(s32[32,1,128]{2,1,0:T(1,128)} %bitcast.23), calls=%async_computation | async-start | bytes 32768 | tf_op jit(solution)/shard_map/all_to_all | solution.py:237
  16.3 4.7 %k1_body.1 = (f32[64,512]{1,0:T(8,128)}, f32[48,1024]{1,0:T(8,128)}) custom-call(s32[24,128]{1,0:T(8,128)} %bitcast.26, s32[24,128]{1,0:T(8,128)} %bitcast.27, s32[24,128]{1,0:T(8,128)} %bitcast.28, bf16[24,128]{1,0:T(8,128)(2,1)} %bitcast.29, s32[1,1024]{1,0:T(1,128)} %bitcast.25), custom_call_target="tpu_custom_call" | custom-call | tf_op jit(solution)/shard_map/k1_body/pallas_call | solution.py:238
  20.9 3.7 %all-to-all-done = s32[32,1,128]{2,1,0:T(1,128)S(1)} async-done(((s32[32,1,128]{2,1,0:T(1,128)}), s32[32,1,128]{2,1,0:T(1,128)S(1)}, u32[]{:S(2)}, u32[]{:S(2)}) %all-to-all-start) | async-done | bytes 16416 | tf_op jit(solution)/shard_map/all_to_all | solution.py:237
  24.7 0.0 copy-start
  24.7 0.6 copy-done
  25.3 2.0 %k2_body.1 = f32[32,16,128]{2,1,0:T(8,128)} custom-call(s32[32,128]{1,0:T(8,128)} %bitcast.21, f32[64,512]{1,0:T(8,128)} %get-tuple-element.8.tab_ref, f32[48,1024]{1,0:T(8,128)} %get-tuple-element.9.cand_ref), custom_call_target="tpu_custom_call" | custom-call | tf_op jit(solution)/shard_map/k2_body/pallas_call | solution.py:250
  27.3 17.8 %all_to_all.15 = f32[32,16,128]{2,1,0:T(8,128)} all-to-all(f32[32,16,128]{2,1,0:T(8,128)} %k2_body.1), channel_id=1, replica_groups=mesh['row_0'=2,'row_1'=8,'col_0'=2,'col_1'=8,'col_2'=2] {'col_0','col_1'..., dimensions={0} | all-to-all | bytes 524288 | tf_op jit(solution)/shard_map/all_to_all | solution.py:251
  45.1 1.7 %k3_body.1 = f32[16,16,128]{2,1,0:T(8,128)} custom-call(f32[512,128]{1,0:T(8,128)} %bitcast.20), custom_call_target="tpu_custom_call" | custom-call | tf_op jit(solution)/shard_map/k3_body/pallas_call | solution.py:252
  46.9 19.3 %all_to_all.16.got_ref = f32[16,16,128]{2,1,0:T(8,128)} all-to-all(f32[16,16,128]{2,1,0:T(8,128)} %k3_body.1), channel_id=1, replica_groups=mesh['row_0'=2,'row_1'=8,'col_0'=2,'col_1'=8,'col_2'=2] {'row_0','row_1'}, dimensions={0} | all-to-all | bytes 262144 | tf_op jit(solution)/shard_map/all_to_all | solution.py:253
  66.2 2.5 %k4_body.1 = (f32[16,128]{1,0:T(8,128)}, f32[8,128]{1,0:T(8,128)}, f32[1,1]{1,0:T(1,128)}) custom-call(s32[2]{0:T(128)} %pad_add_fusion.pos_ref, f32[16,16,128]{2,1,0:T(8,128)} %all_to_all.16.got_ref, s32[32,128]{1,0:T(8,128)} %bitcast.22), custom_call_target="tpu_custom_call" | custom-call | tf_op jit(solution)/shard_map/k4_body/pallas_call | solution.py:254
Async XLA Ops:
  0.6 1.2 %copy-start.1 = (s32[1104]{0:T(1024)S(1)}, s32[1104]{0:T(1024)}, u32[]{:S(2)}) copy-start(s32[1104]{0:T(1024)} %param.11) | copy-start | bytes 13252
  0.7 0.7 copy-start.2
  4.6 20.1 %all-to-all-start = ((s32[32,1,128]{2,1,0:T(1,128)}), s32[32,1,128]{2,1,0:T(1,128)S(1)}, u32[]{:S(2)}, u32[]{:S(2)}) async-start(s32[32,1,128]{2,1,0:T(1,128)} %bitcast.23), calls=%async_computation | async-start | bytes 32768 | tf_op jit(solution)/shard_map/all_to_all | solution.py:237
  24.7 0.6 copy-start

commit v2 on v1

--- a/solution.py
+++ b/solution.py
@@ -47,9 +47,11 @@
     return out
 
 
-def k0_body(pos_ref, words_ref, dates_ref, cands_ref, out_ref):
-    col = pos_ref[0]
-    words = [words_ref[i : i + 1, :] for i in range(9)]
+def k0_body(words_ref, dates_ref, cands_ref, out_ref):
+    col = lax.axis_index(COL)
+    words = [words_ref[i * LANES : (i + 1) * LANES].reshape(1, LANES) for i in range(8)]
+    last = words_ref[8 * LANES : 16 * WORDS].reshape(1, 16 * WORDS - 8 * LANES)
+    words.append(jnp.concatenate([last, jnp.zeros((1, 9 * LANES - 16 * WORDS), I32)], 1))
     cands = cands_ref[...]
     off = jnp.bitwise_and(cands, SUP_DEV - 1)
     block = jnp.right_shift(cands, 11) - 16 * col
@@ -58,14 +60,14 @@
     word = lookup(words, jnp.where(mine, block * WORDS + slot, 0))
     bits = jnp.where(mine, jnp.bitwise_and(jnp.right_shift(word, off - 30 * slot), 1), 0)
     sub, lane = iota((8, LANES), 0), iota((8, LANES), 1)
-    dates = jnp.broadcast_to(dates_ref[...], (8, LANES))
     for j in range(4):
         m = jnp.bitwise_and(4 * sub + j, 15)
         own = lookup(words, jnp.where(lane < WORDS, m * WORDS + lane, 0))
         row = jnp.where(lane < WORDS, own, 0)
         in_bits = (lane >= BITS_AT) & (lane < BITS_AT + 32)
         row = jnp.where(in_bits, roll(bits, BITS_AT - 32 * j), row)
-        row = jnp.where((lane >= DATES_AT) & (lane < DATES_AT + 3), roll(dates, DATES_AT), row)
+        for d in range(3):
+            row = jnp.where(lane == DATES_AT + d, dates_ref[d], row)
         out_ref[pl.ds(j, 8, stride=4), :] = row
 
 
@@ -184,7 +186,7 @@
             out_ref[2 * hi + lo, 8:16, :] = total
 
 
-def k4_body(pos_ref, got_ref, words_ref, owned_ref, cand_ref, total_ref, hi_ref, lo_ref):
+def k4_body(got_ref, words_ref, owned_ref, cand_ref, total_ref, hi_ref, lo_ref):
     lane = iota((8, LANES), 1)
     first = jnp.bitwise_and(lane, 16) == 0
     high, low = iota((16, LANES), 0), iota((LANES, LANES), 0)
@@ -200,7 +202,7 @@
     owned = lax.dot_general(
         hi_ref[...], lo_ref[...], (((1,), (1,)), ((), ())), preferred_element_type=F32
     )
-    words = words_ref[pl.ds(2 * pos_ref[1] + jnp.right_shift(pos_ref[0], 4), 1), :]
+    words = words_ref[pl.ds(2 * lax.axis_index(ROW) + lax.axis_index("col_0"), 1), :]
     place = iota((16, LANES), 0) * LANES + iota((16, LANES), 1)
     slot = div30(place)
     bit = jnp.bitwise_and(jnp.right_shift(lane_gather(words, slot), place - 30 * slot), 1)
@@ -214,7 +216,11 @@
 
 SMEM = pl.BlockSpec(memory_space=pltpu.SMEM)
 VMEM = pl.BlockSpec(memory_space=pltpu.VMEM)
-shape = jax.ShapeDtypeStruct
+shape, here = jax.ShapeDtypeStruct, pltpu.VMEM
+
+
+def near(x):
+    return pltpu.with_memory_space_constraint(x, pltpu.VMEM)
 
 
 def call(body, ins, outs, scratch=(), out_specs=None):
@@ -229,16 +235,16 @@
 
 
 def per_device(fact_block, fact_offset, fact_date, revenue, supplier_words, date_words, candidates):
-    pos = jnp.stack([lax.axis_index(COL), lax.axis_index(ROW)]).astype(I32)
     cands = candidates.reshape(8, LANES)
-    words = jnp.pad(supplier_words, (0, 9 * LANES - 16 * WORDS)).reshape(9, LANES)
-    dates = jnp.pad(date_words, (0, LANES - 3)).reshape(1, LANES)
-    give0 = call(k0_body, [SMEM, VMEM, VMEM, VMEM], shape((NCOL, LANES), I32))(pos, words, dates, cands)
+    give0 = call(k0_body, [VMEM, SMEM, VMEM], here((NCOL, LANES), I32))(
+        supplier_words, date_words, cands
+    )
     got0 = lax.all_to_all(give0.reshape(NCOL, 1, LANES), COL, 0, 0, tiled=True).reshape(NCOL, LANES)
+    got0 = near(got0)
     tab, cand = call(
         k1_body,
         [VMEM] * 5,
-        [shape((64, NDEV), F32), shape((48, 1024), F32)],
+        [here((64, NDEV), F32), here((48, 1024), F32)],
         [pltpu.VMEM((NDEV, CH * LANES), BF16), pltpu.VMEM((80, CH * LANES), BF16)],
     )(
         fact_block.reshape(CH, LANES),
@@ -247,17 +253,19 @@
         revenue.reshape(CH, LANES),
         candidates.reshape(1, 1024),
     )
-    give1 = call(k2_body, [VMEM] * 3, shape((NCOL, 16, LANES), F32), [pltpu.VMEM((8, LANES), F32)])(got0, tab, cand)
+    give1 = call(k2_body, [VMEM] * 3, here((NCOL, 16, LANES), F32), [pltpu.VMEM((8, LANES), F32)])(
+        got0, near(tab), near(cand)
+    )
     got1 = lax.all_to_all(give1, COL, 0, 0, tiled=True)
-    give2 = call(k3_body, [VMEM], shape((NROW, 16, LANES), F32))(got1.reshape(NCOL * 16, LANES))
+    give2 = call(k3_body, [VMEM], here((NROW, 16, LANES), F32))(near(got1.reshape(NCOL * 16, LANES)))
     got2 = lax.all_to_all(give2, ROW, 0, 0, tiled=True)
     owned, cand, total = call(
         k4_body,
-        [SMEM, VMEM, VMEM],
+        [VMEM, VMEM],
         [shape((16, LANES), F32), shape((8, LANES), F32), shape((1, 1), F32)],
         [pltpu.VMEM((16, 64 * LANES), BF16), pltpu.VMEM((LANES, 64 * LANES), BF16)],
         [VMEM, VMEM, SMEM],
-    )(pos, got2, got0)
+    )(near(got2), got0)
     return owned.reshape(SUP_DEV), cand.reshape(1024), total.reshape(())
 
 

time: 69.2 us -> 60.5 us (0.87)
  Pallas kernels: 12.5 us -> 7.63 us
  local copies, waits for them, and re-layouts: 2.37 us -> 0 us
  blocking collectives: 37.2 us -> 35.9 us
    pallas_call x5, Pallas kernels: 12.5 us -> 7.63 us  [the longest x1 4.02 us: per_device(): call(k1_body, [VMEM] * 5, [here((64, NDEV), F32), here((48, 1024), F32)],...]
    unnamed x6 -> x0, local copies, waits for them, and re-layouts: 1.26 us -> none
    reshape x2 -> x0, local copies, waits for them, and re-layouts: 1.11 us -> none  [the longest x1 0.6 us: per_device(): jnp.pad(supplier_words, (0, 9 * LANES - 16 * WORDS)).reshape(9, LANES)]
    all_to_all x1, blocking collectives: 17.8 us -> 16.9 us  [per_device(): got1 = lax.all_to_all(give1, COL, 0, 0, tiled=True)]
where the time goes in v2:
time: 60.5 us; the launch traced here: 60.2 us
  blocking collectives  35.9 us (59%)
  starting transfers between devices  11.6 us (19%)
  Pallas kernels  7.63 us (13%)
  waiting for transfers between devices  4.41 us (7%)
  between operations  0.65 us (1%)
    all_to_all x1, blocking collectives, per_device(): got2 = lax.all_to_all(give2, ROW, 0, 0, tiled=True)  19 us
    all_to_all x1, blocking collectives, per_device(): got1 = lax.all_to_all(give1, COL, 0, 0, tiled=True)  16.9 us
    all_to_all x1, starting transfers between devices, per_device(): lax.all_to_all(give0.reshape(NCOL, 1, LANES), COL, 0, 0, tiled=True)  11.6 us
    all_to_all x1, waiting for transfers between devices, per_device(): lax.all_to_all(give0.reshape(NCOL, 1, LANES), COL, 0, 0, tiled=True)  4.41 us
    pallas_call x1, Pallas kernels, per_device(): call(k1_body, [VMEM] * 5, [here((64, NDEV), F32), here((48, 1024), F32)],...  4.02 us
    pallas_call x1, Pallas kernels, per_device(): call(k4_body, [VMEM, VMEM], [shape((16, LANES), F32), shape((8, LANES), F...  1.62 us
    pallas_call x1, Pallas kernels, per_device(): call(k0_body, [VMEM, SMEM, VMEM], here((NCOL, LANES), I32))  1.57 us
  transfers between devices with their start and end apart: 1, of which 1 were waited for; matrix products, arithmetic and copies ran while one was open for 0% of the time, Pallas kernels for 7%

profile of v2, /device:TPU:8, one launch (start us, length us, event | category | flops | bytes accessed | tf_op | source)
XLA Modules:
  0.0 60.2 jit_solution(14440107070124817814)
XLA Ops:
  0.6 1.6 %k0_body.1 = s32[32,128]{1,0:T(8,128)} custom-call(s32[1104]{0:T(1024)} %words_ref.1, s32[3]{0:T(128)} %dates_ref.1, s32[8,128]{1,0:T(8,128)} %bitcast.17), custom_call_target="tpu_custom_call" | custom-call | tf_op jit(solution)/shard_map/k0_body/pallas_call | solution.py:239
  2.2 11.6 %all-to-all-start = ((s32[32,1,128]{2,1,0:T(1,128)}), s32[32,1,128]{2,1,0:T(1,128)S(1)}, u32[]{:S(2)}, u32[]{:S(2)}) async-start(s32[32,1,128]{2,1,0:T(1,128)} %bitcast.2), calls=%async_computation | async-start | bytes 32768 | tf_op jit(solution)/shard_map/all_to_all | solution.py:242
  13.8 4.0 %k1_body.1 = (f32[64,512]{1,0:T(8,128)S(1)}, f32[48,1024]{1,0:T(8,128)S(1)}) custom-call(s32[24,128]{1,0:T(8,128)} %bitcast.19, s32[24,128]{1,0:T(8,128)} %bitcast.20, s32[24,128]{1,0:T(8,128)} %bitcast.21, bf16[24,128]{1,0:T(8,128)(2,1)} %bitcast.22, s32[1,1024]{1,0:T(1,128)} %bitcast.18), custom_call_target="tpu_custom_call" | custom-call | tf_op jit(solution)/shard_map/k1_body/pallas_call | solution.py:244
  17.9 4.4 %all-to-all-done = s32[32,1,128]{2,1,0:T(1,128)S(1)} async-done(((s32[32,1,128]{2,1,0:T(1,128)}), s32[32,1,128]{2,1,0:T(1,128)S(1)}, u32[]{:S(2)}, u32[]{:S(2)}) %all-to-all-start) | async-done | bytes 16416 | tf_op jit(solution)/shard_map/all_to_all | solution.py:242
  22.3 0.3 k2_body.1
  22.6 16.9 %all_to_all.15 = f32[32,16,128]{2,1,0:T(8,128)S(1)} all-to-all(f32[32,16,128]{2,1,0:T(8,128)S(1)} %k2_body.1), channel_id=1, replica_groups=mesh['row_0'=2,'row_1'=8,'col_0'=2,'col_1'=8,'col_2'=2] {'col_0','col_1'..., dimensions={0} | all-to-all | bytes 524288 | tf_op jit(solution)/shard_map/all_to_all | solution.py:259
  39.4 0.1 k3_body.1
  39.6 19.0 %all_to_all.16.got_ref = f32[16,16,128]{2,1,0:T(8,128)S(1)} all-to-all(f32[16,16,128]{2,1,0:T(8,128)S(1)} %k3_body.1), channel_id=1, replica_groups=mesh['row_0'=2,'row_1'=8,'col_0'=2,'col_1'=8,'col_2'=2] {'row_0','row_1'}, dimensions={0} | all-to-all | bytes 262144 | tf_op jit(solution)/shard_map/all_to_all | solution.py:261
  58.6 1.6 %k4_body.1 = (f32[16,128]{1,0:T(8,128)}, f32[8,128]{1,0:T(8,128)}, f32[1,1]{1,0:T(1,128)}) custom-call(f32[16,16,128]{2,1,0:T(8,128)S(1)} %all_to_all.16.got_ref, s32[32,128]{1,0:T(8,128)S(1)} %bitcast.16), custom_call_target="tpu_custom_call" | custom-call | tf_op jit(solution)/shard_map/k4_body/pallas_call | solution.py:262
Async XLA Ops:
  2.2 20.1 %all-to-all-start = ((s32[32,1,128]{2,1,0:T(1,128)}), s32[32,1,128]{2,1,0:T(1,128)S(1)}, u32[]{:S(2)}, u32[]{:S(2)}) async-start(s32[32,1,128]{2,1,0:T(1,128)} %bitcast.2), calls=%async_computation | async-start | bytes 32768 | tf_op jit(solution)/shard_map/all_to_all | solution.py:242

commit v3 on v2

--- a/solution.py
+++ b/solution.py
@@ -19,6 +19,7 @@
 CH = 24
 F32, BF16, I32 = jnp.float32, jnp.bfloat16, jnp.int32
 BITS_AT, DATES_AT = 72, 104
+GIVE = 12
 
 
 def iota(shape, dim):
@@ -77,9 +78,9 @@
 
     def key_of(b):
         return (
-            jnp.bitwise_and(jnp.right_shift(b, 5), 1) * 256
-            + jnp.bitwise_and(b, 31) * 8
-            + jnp.right_shift(b, 6)
+            jnp.bitwise_and(jnp.right_shift(b, 5), 3) * LANES
+            + jnp.bitwise_and(b, 31) * 4
+            + jnp.right_shift(b, 7)
         )
 
     key = key_of(block)
@@ -138,9 +139,11 @@
         table = jnp.where(lane == 32 * j + src, word, table)
     table = jnp.sum(table, axis=0, keepdims=True)
     bits = jnp.sum(got, axis=0, keepdims=True)
-    bits = roll(jnp.broadcast_to(bits, (8, LANES)), 64 - BITS_AT).astype(F32)
+    row, at_lane = iota((LANES, LANES), 0), iota((LANES, LANES), 1)
+    spare = (jnp.bitwise_and(row, 3) == 0) & (jnp.bitwise_and(at_lane, 15) >= 12)
     lane8 = iota((8, LANES), 1)
-    bits = jnp.where((iota((8, LANES), 0) == 0) & (lane8 >= 64) & (lane8 < 96), bits, 0.0)
+    source = BITS_AT + 4 * jnp.right_shift(lane8, 4) + jnp.bitwise_and(lane8, 3)
+    bits = lane_gather(bits, source).astype(F32)[0:1]
 
     def date_ok(where, place):
         return jnp.bitwise_and(jnp.right_shift(lane_gather(table, where.astype(I32)), place.astype(I32)), 1) == 1
@@ -155,35 +158,35 @@
         at = slice(i * LANES, (i + 1) * LANES)
         keep = date_ok(tab_ref[32:48, at], tab_ref[48:64, at])
         kept.append(jnp.where(keep, tab_ref[16:32, at], 0.0))
-    for h in range(2):
-        at, also = slice(h * LANES, (h + 1) * LANES), slice((h + 2) * LANES, (h + 3) * LANES)
-        stack = jnp.concatenate(
-            [tab_ref[0:16, at], kept[h], tab_ref[0:16, also], kept[h + 2], jnp.zeros((64, LANES), F32)], 0
-        )
-        tiles = jnp.transpose(stack)
-        for t in range(16):
-            out_ref[16 * h + t, 0:8, :] = tiles[8 * t : 8 * t + 8] + bits
-            out_ref[16 * h + t, 8:16, :] = part
+    stack = []
+    for i in range(4):
+        stack += [tab_ref[0:16, i * LANES : (i + 1) * LANES], kept[i]]
+    tiles = jnp.where(spare, bits, jnp.transpose(jnp.concatenate(stack, 0)))
+    for c in range(NCOL):
+        out_ref[GIVE * c : GIVE * c + 4, :] = tiles[4 * c : 4 * c + 4]
+        out_ref[GIVE * c + 4 : GIVE * c + 12, :] = part
 
 
 def k3_body(got_ref, out_ref):
     lane = iota((8, LANES), 1)
+    source = 16 * jnp.right_shift(jnp.bitwise_and(lane, 31), 2) + 12 + jnp.bitwise_and(lane, 3)
     bits = jnp.zeros((8, LANES), F32)
     for j in range(4):
-        rows = roll(got_ref[pl.ds(16 * j, 8, stride=64), :], 32 * j - 64)
+        rows = got_ref[pl.ds(GIVE * j, 8, stride=4 * GIVE), :]
+        rows = jnp.take_along_axis(rows, source, axis=1, mode="promise_in_bounds")
         bits = jnp.where(jnp.right_shift(lane, 5) == j, rows, bits)
-    total = got_ref[8:16, :]
+    total = got_ref[4:12, :]
     for c in range(1, NCOL):
-        total = total + got_ref[16 * c + 8 : 16 * c + 16, :]
+        total = total + got_ref[GIVE * c + 4 : GIVE * c + 12, :]
     total = total * bits
-    for hi in range(8):
-        rows = got_ref[pl.ds(hi, NCOL, stride=16), :]
-        for lo in range(2):
+    for hi in range(4):
+        rows = got_ref[pl.ds(hi, NCOL, stride=GIVE), :]
+        for lo in range(4):
             tile = roll(rows[0:8], -32 * lo)
             for q in range(1, 4):
                 tile = jnp.where(jnp.right_shift(lane, 5) == q, roll(rows[8 * q : 8 * q + 8], 32 * (q - lo)), tile)
-            out_ref[2 * hi + lo, 0:8, :] = tile
-            out_ref[2 * hi + lo, 8:16, :] = total
+            out_ref[4 * hi + lo, 0:8, :] = jnp.where(jnp.bitwise_and(lane, 15) < 12, tile, 0.0)
+            out_ref[4 * hi + lo, 8:16, :] = total
 
 
 def k4_body(got_ref, words_ref, owned_ref, cand_ref, total_ref, hi_ref, lo_ref):
@@ -253,11 +256,11 @@
         revenue.reshape(CH, LANES),
         candidates.reshape(1, 1024),
     )
-    give1 = call(k2_body, [VMEM] * 3, here((NCOL, 16, LANES), F32), [pltpu.VMEM((8, LANES), F32)])(
+    give1 = call(k2_body, [VMEM] * 3, here((NCOL * GIVE, LANES), F32), [pltpu.VMEM((8, LANES), F32)])(
         got0, near(tab), near(cand)
     )
-    got1 = lax.all_to_all(give1, COL, 0, 0, tiled=True)
-    give2 = call(k3_body, [VMEM], here((NROW, 16, LANES), F32))(near(got1.reshape(NCOL * 16, LANES)))
+    got1 = lax.all_to_all(give1.reshape(NCOL, 1, GIVE * LANES), COL, 0, 0, tiled=True)
+    give2 = call(k3_body, [VMEM], here((NROW, 16, LANES), F32))(near(got1.reshape(NCOL * GIVE, LANES)))
     got2 = lax.all_to_all(give2, ROW, 0, 0, tiled=True)
     owned, cand, total = call(
         k4_body,

time: 60.5 us -> 59 us (0.975)
  blocking collectives: 35.9 us -> 34.4 us
    all_to_all x1, blocking collectives: 16.9 us -> 15.5 us  [per_device(): lax.all_to_all(give1.reshape(NCOL, 1, GIVE * LANES), COL, 0, 0, tiled=True)]
where the time goes in v3:
time: 59 us; the launch traced here: 58.7 us
  blocking collectives  34.4 us (58%)
  starting transfers between devices  11.6 us (20%)
  Pallas kernels  7.6 us (13%)
  waiting for transfers between devices  4.41 us (7%)
  between operations  0.66 us (1%)
    all_to_all x1, blocking collectives, per_device(): got2 = lax.all_to_all(give2, ROW, 0, 0, tiled=True)  18.9 us
    all_to_all x1, blocking collectives, per_device(): lax.all_to_all(give1.reshape(NCOL, 1, GIVE * LANES), COL, 0, 0, tiled=True)  15.5 us
    all_to_all x1, starting transfers between devices, per_device(): lax.all_to_all(give0.reshape(NCOL, 1, LANES), COL, 0, 0, tiled=True)  11.6 us
    all_to_all x1, waiting for transfers between devices, per_device(): lax.all_to_all(give0.reshape(NCOL, 1, LANES), COL, 0, 0, tiled=True)  4.41 us
    pallas_call x1, Pallas kernels, per_device(): call(k1_body, [VMEM] * 5, [here((64, NDEV), F32), here((48, 1024), F32)],...  4.02 us
    pallas_call x1, Pallas kernels, per_device(): call(k4_body, [VMEM, VMEM], [shape((16, LANES), F32), shape((8, LANES), F...  1.62 us
    pallas_call x1, Pallas kernels, per_device(): call(k0_body, [VMEM, SMEM, VMEM], here((NCOL, LANES), I32))  1.57 us
  transfers between devices with their start and end apart: 1, of which 1 were waited for; matrix products, arithmetic and copies ran while one was open for 0% of the time, Pallas kernels for 7%

profile of v3, /device:TPU:8, one launch (start us, length us, event | category | flops | bytes accessed | tf_op | source)
XLA Modules:
  0.0 58.7 jit_solution(7678279170724515011)
XLA Ops:
  0.6 1.6 %k0_body.1 = s32[32,128]{1,0:T(8,128)} custom-call(s32[1104]{0:T(1024)} %words_ref.1, s32[3]{0:T(128)} %dates_ref.1, s32[8,128]{1,0:T(8,128)} %bitcast.19), custom_call_target="tpu_custom_call" | custom-call | tf_op jit(solution)/shard_map/k0_body/pallas_call | solution.py:242
  2.2 11.6 %all-to-all-start = ((s32[32,1,128]{2,1,0:T(1,128)}), s32[32,1,128]{2,1,0:T(1,128)S(1)}, u32[]{:S(2)}, u32[]{:S(2)}) async-start(s32[32,1,128]{2,1,0:T(1,128)} %bitcast.2), calls=%async_computation | async-start | bytes 32768 | tf_op jit(solution)/shard_map/all_to_all | solution.py:245
  13.8 4.0 %k1_body.1 = (f32[64,512]{1,0:T(8,128)S(1)}, f32[48,1024]{1,0:T(8,128)S(1)}) custom-call(s32[24,128]{1,0:T(8,128)} %bitcast.21, s32[24,128]{1,0:T(8,128)} %bitcast.22, s32[24,128]{1,0:T(8,128)} %bitcast.23, bf16[24,128]{1,0:T(8,128)(2,1)} %bitcast.24, s32[1,1024]{1,0:T(1,128)} %bitcast.20), custom_call_target="tpu_custom_call" | custom-call | tf_op jit(solution)/shard_map/k1_body/pallas_call | solution.py:247
  17.9 4.4 %all-to-all-done = s32[32,1,128]{2,1,0:T(1,128)S(1)} async-done(((s32[32,1,128]{2,1,0:T(1,128)}), s32[32,1,128]{2,1,0:T(1,128)S(1)}, u32[]{:S(2)}, u32[]{:S(2)}) %all-to-all-start) | async-done | bytes 16416 | tf_op jit(solution)/shard_map/all_to_all | solution.py:245
  22.3 0.3 k2_body.1
  22.6 15.5 %all_to_all.15 = f32[32,1,1536]{2,1,0:T(1,128)S(1)} all-to-all(f32[32,1,1536]{2,1,0:T(1,128)S(1)} %bitcast.15), channel_id=1, replica_groups=mesh['row_0'=2,'row_1'=8,'col_0'=2,'col_1'=8,'col_2'=2] {'col_0','col_1'..., dimensions={0} | all-to-all | bytes 393216 | tf_op jit(solution)/shard_map/all_to_all | solution.py:262
  38.0 0.1 k3_body.1
  38.2 18.9 %all_to_all.16.got_ref = f32[16,16,128]{2,1,0:T(8,128)S(1)} all-to-all(f32[16,16,128]{2,1,0:T(8,128)S(1)} %k3_body.1), channel_id=1, replica_groups=mesh['row_0'=2,'row_1'=8,'col_0'=2,'col_1'=8,'col_2'=2] {'row_0','row_1'}, dimensions={0} | all-to-all | bytes 262144 | tf_op jit(solution)/shard_map/all_to_all | solution.py:264
  57.1 1.6 %k4_body.1 = (f32[16,128]{1,0:T(8,128)}, f32[8,128]{1,0:T(8,128)}, f32[1,1]{1,0:T(1,128)}) custom-call(f32[16,16,128]{2,1,0:T(8,128)S(1)} %all_to_all.16.got_ref, s32[32,128]{1,0:T(8,128)S(1)} %bitcast.18), custom_call_target="tpu_custom_call" | custom-call | tf_op jit(solution)/shard_map/k4_body/pallas_call | solution.py:265
Async XLA Ops:
  2.2 20.1 %all-to-all-start = ((s32[32,1,128]{2,1,0:T(1,128)}), s32[32,1,128]{2,1,0:T(1,128)S(1)}, u32[]{:S(2)}, u32[]{:S(2)}) async-start(s32[32,1,128]{2,1,0:T(1,128)} %bitcast.2), calls=%async_computation | async-start | bytes 32768 | tf_op jit(solution)/shard_map/all_to_all | solution.py:245

commit v4 on v3

--- a/solution.py
+++ b/solution.py
@@ -11,15 +11,17 @@
 ROW = ("row_0", "row_1")
 COL = ("col_0", "col_1", "col_2")
 ROW_COL = ROW + COL
-
-NROW, NCOL, NDEV = 16, 32, 512
+NEAR = ("col_1", "col_2")
+FAR = ("row_0", "row_1", "col_0")
+
+NNEAR, NFAR, NCOL, NDEV = 16, 32, 32, 512
 SUP_DEV = 2048
 WORDS = 69
 LANES = 128
 CH = 24
 F32, BF16, I32 = jnp.float32, jnp.bfloat16, jnp.int32
-BITS_AT, DATES_AT = 72, 104
-GIVE = 12
+DATES_AT = 104
+LAST = 12
 
 
 def iota(shape, dim):
@@ -48,7 +50,7 @@
     return out
 
 
-def k0_body(words_ref, dates_ref, cands_ref, out_ref):
+def k0_body(words_ref, dates_ref, cands_ref, out_ref, bits_ref):
     col = lax.axis_index(COL)
     words = [words_ref[i * LANES : (i + 1) * LANES].reshape(1, LANES) for i in range(8)]
     last = words_ref[8 * LANES : 16 * WORDS].reshape(1, 16 * WORDS - 8 * LANES)
@@ -60,16 +62,17 @@
     slot = div30(off)
     word = lookup(words, jnp.where(mine, block * WORDS + slot, 0))
     bits = jnp.where(mine, jnp.bitwise_and(jnp.right_shift(word, off - 30 * slot), 1), 0)
+    bits_ref[0:8, :] = bits
+    bits_ref[8:16, :] = bits
     sub, lane = iota((8, LANES), 0), iota((8, LANES), 1)
     for j in range(4):
         m = jnp.bitwise_and(4 * sub + j, 15)
         own = lookup(words, jnp.where(lane < WORDS, m * WORDS + lane, 0))
         row = jnp.where(lane < WORDS, own, 0)
-        in_bits = (lane >= BITS_AT) & (lane < BITS_AT + 32)
-        row = jnp.where(in_bits, roll(bits, BITS_AT - 32 * j), row)
         for d in range(3):
             row = jnp.where(lane == DATES_AT + d, dates_ref[d], row)
-        out_ref[pl.ds(j, 8, stride=4), :] = row
+        out_ref[pl.ds(2 * j, 8, stride=8), :] = row
+        out_ref[pl.ds(2 * j + 1, 8, stride=8), :] = roll(bits_ref[pl.ds(j // 2, 8, stride=2), :], 64 * (j % 2))
 
 
 def k1_body(block_ref, off_ref, date_ref, rev_ref, cands_ref, tab_ref, cand_ref, hot_ref, val_ref):
@@ -78,9 +81,9 @@
 
     def key_of(b):
         return (
-            jnp.bitwise_and(jnp.right_shift(b, 5), 3) * LANES
-            + jnp.bitwise_and(b, 31) * 4
-            + jnp.right_shift(b, 7)
+            jnp.bitwise_and(jnp.right_shift(b, 4), 3) * LANES
+            + jnp.bitwise_and(b, 15) * 8
+            + jnp.right_shift(b, 6)
         )
 
     key = key_of(block)
@@ -131,19 +134,19 @@
 
 
 def k2_body(got_ref, tab_ref, cand_ref, out_ref, tmp_ref):
-    got = got_ref[...]
+    got = got_ref[pl.ds(0, NCOL, stride=2), :]
     src, lane = iota((NCOL, LANES), 0), iota((NCOL, LANES), 1)
     table = jnp.zeros((NCOL, LANES), I32)
     for j in range(3):
         word = jnp.broadcast_to(got[:, DATES_AT + j : DATES_AT + j + 1], (NCOL, LANES))
         table = jnp.where(lane == 32 * j + src, word, table)
     table = jnp.sum(table, axis=0, keepdims=True)
-    bits = jnp.sum(got, axis=0, keepdims=True)
+    bits = jnp.sum(got_ref[pl.ds(1, NCOL, stride=2), :], axis=0, keepdims=True)
     row, at_lane = iota((LANES, LANES), 0), iota((LANES, LANES), 1)
-    spare = (jnp.bitwise_and(row, 3) == 0) & (jnp.bitwise_and(at_lane, 15) >= 12)
+    row = jnp.where(jnp.bitwise_and(at_lane, 15) >= 12, jnp.bitwise_and(row, 7), 7)
     lane8 = iota((8, LANES), 1)
-    source = BITS_AT + 4 * jnp.right_shift(lane8, 4) + jnp.bitwise_and(lane8, 3)
-    bits = lane_gather(bits, source).astype(F32)[0:1]
+    source = 4 * jnp.right_shift(lane8, 4) + jnp.bitwise_and(lane8, 3)
+    bits = [lane_gather(bits, source + 32 * i).astype(F32)[0:1] for i in range(2)]
 
     def date_ok(where, place):
         return jnp.bitwise_and(jnp.right_shift(lane_gather(table, where.astype(I32)), place.astype(I32)), 1) == 1
@@ -161,10 +164,11 @@
     stack = []
     for i in range(4):
         stack += [tab_ref[0:16, i * LANES : (i + 1) * LANES], kept[i]]
-    tiles = jnp.where(spare, bits, jnp.transpose(jnp.concatenate(stack, 0)))
-    for c in range(NCOL):
-        out_ref[GIVE * c : GIVE * c + 4, :] = tiles[4 * c : 4 * c + 4]
-        out_ref[GIVE * c + 4 : GIVE * c + 12, :] = part
+    tiles = jnp.transpose(jnp.concatenate(stack, 0))
+    tiles = jnp.where(row == 0, bits[0], jnp.where(row == 1, bits[1], tiles))
+    for g in range(NNEAR):
+        out_ref[16 * g : 16 * g + 8, :] = tiles[8 * g : 8 * g + 8]
+        out_ref[16 * g + 8 : 16 * g + 16, :] = part
 
 
 def k3_body(got_ref, out_ref):
@@ -172,32 +176,36 @@
     source = 16 * jnp.right_shift(jnp.bitwise_and(lane, 31), 2) + 12 + jnp.bitwise_and(lane, 3)
     bits = jnp.zeros((8, LANES), F32)
     for j in range(4):
-        rows = got_ref[pl.ds(GIVE * j, 8, stride=4 * GIVE), :]
+        rows = got_ref[pl.ds(16 * (j // 2) + j % 2, 8, stride=32), :]
         rows = jnp.take_along_axis(rows, source, axis=1, mode="promise_in_bounds")
         bits = jnp.where(jnp.right_shift(lane, 5) == j, rows, bits)
-    total = got_ref[4:12, :]
-    for c in range(1, NCOL):
-        total = total + got_ref[GIVE * c + 4 : GIVE * c + 12, :]
+    total = got_ref[8:16, :]
+    for g in range(1, NNEAR):
+        total = total + got_ref[16 * g + 8 : 16 * g + 16, :]
     total = total * bits
-    for hi in range(4):
-        rows = got_ref[pl.ds(hi, NCOL, stride=GIVE), :]
+    lane = iota((4, LANES), 1)
+    for hi in range(8):
+        rows = [got_ref[pl.ds(64 * q + hi, 4, stride=16), :] for q in range(4)]
         for lo in range(4):
-            tile = roll(rows[0:8], -32 * lo)
+            tile = roll(rows[0], -32 * lo)
             for q in range(1, 4):
-                tile = jnp.where(jnp.right_shift(lane, 5) == q, roll(rows[8 * q : 8 * q + 8], 32 * (q - lo)), tile)
-            out_ref[4 * hi + lo, 0:8, :] = jnp.where(jnp.bitwise_and(lane, 15) < 12, tile, 0.0)
-            out_ref[4 * hi + lo, 8:16, :] = total
+                tile = jnp.where(jnp.right_shift(lane, 5) == q, roll(rows[q], 32 * (q - lo)), tile)
+            at = LAST * (4 * hi + lo)
+            out_ref[at : at + 4, :] = jnp.where(jnp.bitwise_and(lane, 15) < 12, tile, 0.0)
+            out_ref[at + 4 : at + 12, :] = total
 
 
 def k4_body(got_ref, words_ref, owned_ref, cand_ref, total_ref, hi_ref, lo_ref):
     lane = iota((8, LANES), 1)
     first = jnp.bitwise_and(lane, 16) == 0
-    high, low = iota((16, LANES), 0), iota((LANES, LANES), 0)
+    high, low = iota((32, LANES), 0), iota((64, LANES), 0)
+    high = 2 * jnp.bitwise_and(high, 15) + jnp.right_shift(high, 4)
     for p in range(8):
-        even, odd = got_ref[2 * p, 0:8, :], got_ref[2 * p + 1, 0:8, :]
+        even = got_ref[pl.ds(16 * LAST * (p // 4) + p % 4, 8, stride=LAST), :]
+        odd = got_ref[pl.ds(16 * LAST * (p // 4) + 8 * LAST + p % 4, 8, stride=LAST), :]
         off = jnp.where(first, even, roll(odd, 16)).astype(I32)
         rev = jnp.where(first, roll(even, -16), odd)
-        off_hi, off_lo = jnp.right_shift(off, 7), jnp.bitwise_and(off, 127)
+        off_hi, off_lo = jnp.right_shift(off, 6), jnp.bitwise_and(off, 63)
         for s in range(8):
             at = slice((8 * p + s) * LANES, (8 * p + s + 1) * LANES)
             hi_ref[:, at] = jnp.where(off_hi[s : s + 1] == high, rev[s : s + 1], 0.0).astype(BF16)
@@ -205,14 +213,15 @@
     owned = lax.dot_general(
         hi_ref[...], lo_ref[...], (((1,), (1,)), ((), ())), preferred_element_type=F32
     )
-    words = words_ref[pl.ds(2 * lax.axis_index(ROW) + lax.axis_index("col_0"), 1), :]
+    owned = jnp.concatenate([owned[0:16], owned[16:32]], 1)
+    words = words_ref[pl.ds(2 * lax.axis_index(FAR), 1), :]
     place = iota((16, LANES), 0) * LANES + iota((16, LANES), 1)
     slot = div30(place)
     bit = jnp.bitwise_and(jnp.right_shift(lane_gather(words, slot), place - 30 * slot), 1)
     owned_ref[...] = jnp.where(bit == 1, owned, 0.0)
-    cand = got_ref[0, 8:16, :]
-    for r in range(1, NROW):
-        cand = cand + got_ref[r, 8:16, :]
+    cand = got_ref[4:12, :]
+    for h in range(1, NFAR):
+        cand = cand + got_ref[LAST * h + 4 : LAST * h + 12, :]
     cand_ref[...] = cand
     total_ref[0, 0] = jnp.sum(cand)
 
@@ -239,11 +248,11 @@
 
 def per_device(fact_block, fact_offset, fact_date, revenue, supplier_words, date_words, candidates):
     cands = candidates.reshape(8, LANES)
-    give0 = call(k0_body, [VMEM, SMEM, VMEM], here((NCOL, LANES), I32))(
+    give0 = call(k0_body, [VMEM, SMEM, VMEM], here((2 * NCOL, LANES), I32), [pltpu.VMEM((16, LANES), I32)])(
         supplier_words, date_words, cands
     )
-    got0 = lax.all_to_all(give0.reshape(NCOL, 1, LANES), COL, 0, 0, tiled=True).reshape(NCOL, LANES)
-    got0 = near(got0)
+    got0 = lax.all_to_all(give0.reshape(NCOL, 1, 2 * LANES), COL, 0, 0, tiled=True)
+    got0 = near(got0.reshape(2 * NCOL, LANES))
     tab, cand = call(
         k1_body,
         [VMEM] * 5,
@@ -256,17 +265,18 @@
         revenue.reshape(CH, LANES),
         candidates.reshape(1, 1024),
     )
-    give1 = call(k2_body, [VMEM] * 3, here((NCOL * GIVE, LANES), F32), [pltpu.VMEM((8, LANES), F32)])(
+    give1 = call(k2_body, [VMEM] * 3, here((NNEAR * 16, LANES), F32), [pltpu.VMEM((8, LANES), F32)])(
         got0, near(tab), near(cand)
     )
-    got1 = lax.all_to_all(give1.reshape(NCOL, 1, GIVE * LANES), COL, 0, 0, tiled=True)
-    give2 = call(k3_body, [VMEM], here((NROW, 16, LANES), F32))(near(got1.reshape(NCOL * GIVE, LANES)))
-    got2 = lax.all_to_all(give2, ROW, 0, 0, tiled=True)
+    got1 = lax.all_to_all(give1.reshape(NNEAR, 1, 16 * LANES), NEAR, 0, 0, tiled=True)
+    give2 = call(k3_body, [VMEM], here((NFAR * LAST, LANES), F32))(near(got1.reshape(NNEAR * 16, LANES)))
+    got2 = lax.all_to_all(give2.reshape(NFAR, 1, LAST * LANES), FAR, 0, 0, tiled=True)
+    got2 = got2.reshape(NFAR * LAST, LANES)
     owned, cand, total = call(
         k4_body,
         [VMEM, VMEM],
         [shape((16, LANES), F32), shape((8, LANES), F32), shape((1, 1), F32)],
-        [pltpu.VMEM((16, 64 * LANES), BF16), pltpu.VMEM((LANES, 64 * LANES), BF16)],
+        [pltpu.VMEM((32, 64 * LANES), BF16), pltpu.VMEM((64, 64 * LANES), BF16)],
         [VMEM, VMEM, SMEM],
     )(near(got2), got0)
     return owned.reshape(SUP_DEV), cand.reshape(1024), total.reshape(())

time: 59 us -> 58.8 us (level)
  the two profiles are of different devices: /device:TPU:8 before, /device:TPU:1 now
where the time goes in v4:
time: 58.8 us; the launch traced here: 58.5 us
  blocking collectives  33.6 us (57%)
  starting transfers between devices  12.9 us (22%)
  Pallas kernels  7.47 us (13%)
  waiting for transfers between devices  3.92 us (7%)
  between operations  0.66 us (1%)
    all_to_all x1, blocking collectives, per_device(): lax.all_to_all(give2.reshape(NFAR, 1, LAST * LANES), FAR, 0, 0, tiled=True)  21.1 us
    all_to_all x1, starting transfers between devices, per_device(): lax.all_to_all(give0.reshape(NCOL, 1, 2 * LANES), COL, 0, 0, tiled=True)  12.9 us
    all_to_all x1, blocking collectives, per_device(): lax.all_to_all(give1.reshape(NNEAR, 1, 16 * LANES), NEAR, 0, 0, tiled=True)  12.5 us
    pallas_call x1, Pallas kernels, per_device(): call(k1_body, [VMEM] * 5, [here((64, NDEV), F32), here((48, 1024), F32)],...  4.02 us
    all_to_all x1, waiting for transfers between devices, per_device(): lax.all_to_all(give0.reshape(NCOL, 1, 2 * LANES), COL, 0, 0, tiled=True)  3.92 us
    pallas_call x1, Pallas kernels, per_device(): call(k0_body, [VMEM, SMEM, VMEM], here((2 * NCOL, LANES), I32), [pltpu.VM...  1.57 us
    pallas_call x1, Pallas kernels, per_device(): call(k4_body, [VMEM, VMEM], [shape((16, LANES), F32), shape((8, LANES), F...  1.43 us
  transfers between devices with their start and end apart: 1, of which 1 were waited for; matrix products, arithmetic and copies ran while one was open for 0% of the time, Pallas kernels for 7%

profile of v4, /device:TPU:1, one launch (start us, length us, event | category | flops | bytes accessed | tf_op | source)
XLA Modules:
  0.0 58.5 jit_solution(6838550142044320500)
XLA Ops:
  0.6 1.6 %k0_body.1 = s32[64,128]{1,0:T(8,128)} custom-call(s32[1104]{0:T(1024)} %words_ref.1, s32[3]{0:T(128)} %dates_ref.1, s32[8,128]{1,0:T(8,128)} %bitcast.21), custom_call_target="tpu_custom_call" | custom-call | tf_op jit(solution)/shard_map/k0_body/pallas_call | solution.py:251
  2.2 12.9 %all-to-all-start = ((s32[32,1,256]{2,1,0:T(1,128)}), s32[32,1,256]{2,1,0:T(1,128)S(1)}, u32[]{:S(2)}, u32[]{:S(2)}) async-start(s32[32,1,256]{2,1,0:T(1,128)} %bitcast.1), calls=%async_computation | async-start | bytes 65536 | tf_op jit(solution)/shard_map/all_to_all | solution.py:254
  15.1 4.0 %k1_body.1 = (f32[64,512]{1,0:T(8,128)S(1)}, f32[48,1024]{1,0:T(8,128)S(1)}) custom-call(s32[24,128]{1,0:T(8,128)} %bitcast.23, s32[24,128]{1,0:T(8,128)} %bitcast.24, s32[24,128]{1,0:T(8,128)} %bitcast.25, bf16[24,128]{1,0:T(8,128)(2,1)} %bitcast.26, s32[1,1024]{1,0:T(1,128)} %bitcast.22), custom_call_target="tpu_custom_call" | custom-call | tf_op jit(solution)/shard_map/k1_body/pallas_call | solution.py:256
  19.1 3.9 %all-to-all-done = s32[32,1,256]{2,1,0:T(1,128)S(1)} async-done(((s32[32,1,256]{2,1,0:T(1,128)}), s32[32,1,256]{2,1,0:T(1,128)S(1)}, u32[]{:S(2)}, u32[]{:S(2)}) %all-to-all-start) | async-done | bytes 32800 | tf_op jit(solution)/shard_map/all_to_all | solution.py:254
  23.0 0.3 k2_body.1
  23.3 12.5 %all_to_all.15 = f32[16,1,2048]{2,1,0:T(1,128)S(1)} all-to-all(f32[16,1,2048]{2,1,0:T(1,128)S(1)} %bitcast.18), channel_id=1, replica_groups=mesh['row_0'=2,'row_1'=8,'col_0'=2,'col_1'=8,'col_2'=2] {'col_1','col_2'}, dimensions={0} | all-to-all | bytes 262144 | tf_op jit(solution)/shard_map/all_to_all | solution.py:271
  35.8 0.2 k3_body.1
  36.0 21.1 %all_to_all.16 = f32[32,1,1536]{2,1,0:T(1,128)S(1)} all-to-all(f32[32,1,1536]{2,1,0:T(1,128)S(1)} %bitcast.16), channel_id=1, replica_groups=mesh['row_0'=2,'row_1'=8,'col_0'=2,'col_1'=8,'col_2'=2] {'row_0','row_1'..., dimensions={0} | all-to-all | bytes 393216 | tf_op jit(solution)/shard_map/all_to_all | solution.py:273
  57.1 1.4 %k4_body.1 = (f32[16,128]{1,0:T(8,128)}, f32[8,128]{1,0:T(8,128)}, f32[1,1]{1,0:T(1,128)}) custom-call(f32[384,128]{1,0:T(8,128)S(1)} %bitcast.15, s32[64,128]{1,0:T(8,128)S(1)} %bitcast.20), custom_call_target="tpu_custom_call" | custom-call | tf_op jit(solution)/shard_map/k4_body/pallas_call | solution.py:275
Async XLA Ops:
  2.2 20.8 %all-to-all-start = ((s32[32,1,256]{2,1,0:T(1,128)}), s32[32,1,256]{2,1,0:T(1,128)S(1)}, u32[]{:S(2)}, u32[]{:S(2)}) async-start(s32[32,1,256]{2,1,0:T(1,128)} %bitcast.1), calls=%async_computation | async-start | bytes 65536 | tf_op jit(solution)/shard_map/all_to_all | solution.py:254

commit v5 on v4

--- a/solution.py
+++ b/solution.py
@@ -172,17 +172,9 @@
 
 
 def k3_body(got_ref, out_ref):
-    lane = iota((8, LANES), 1)
-    source = 16 * jnp.right_shift(jnp.bitwise_and(lane, 31), 2) + 12 + jnp.bitwise_and(lane, 3)
-    bits = jnp.zeros((8, LANES), F32)
-    for j in range(4):
-        rows = got_ref[pl.ds(16 * (j // 2) + j % 2, 8, stride=32), :]
-        rows = jnp.take_along_axis(rows, source, axis=1, mode="promise_in_bounds")
-        bits = jnp.where(jnp.right_shift(lane, 5) == j, rows, bits)
     total = got_ref[8:16, :]
     for g in range(1, NNEAR):
         total = total + got_ref[16 * g + 8 : 16 * g + 16, :]
-    total = total * bits
     lane = iota((4, LANES), 1)
     for hi in range(8):
         rows = [got_ref[pl.ds(64 * q + hi, 4, stride=16), :] for q in range(4)]
@@ -195,7 +187,25 @@
             out_ref[at + 4 : at + 12, :] = total
 
 
-def k4_body(got_ref, words_ref, owned_ref, cand_ref, total_ref, hi_ref, lo_ref):
+def kb_body(got_ref, out_ref):
+    lane = iota((8, LANES), 1)
+    source = 16 * jnp.right_shift(jnp.bitwise_and(lane, 31), 2) + 12 + jnp.bitwise_and(lane, 3)
+    bits = jnp.zeros((8, LANES), F32)
+    for j in range(4):
+        rows = got_ref[pl.ds(16 * (j // 2) + j % 2, 8, stride=32), :]
+        rows = jnp.take_along_axis(rows, source, axis=1, mode="promise_in_bounds")
+        bits = jnp.where(jnp.right_shift(lane, 5) == j, rows, bits)
+    out_ref[...] = bits
+
+
+def ka_body(words_ref, out_ref):
+    words = words_ref[pl.ds(2 * lax.axis_index(FAR), 1), :]
+    place = iota((16, LANES), 0) * LANES + iota((16, LANES), 1)
+    slot = div30(place)
+    out_ref[...] = jnp.bitwise_and(jnp.right_shift(lane_gather(words, slot), place - 30 * slot), 1)
+
+
+def k4_body(got_ref, own_ref, bits_ref, owned_ref, cand_ref, total_ref, hi_ref, lo_ref):
     lane = iota((8, LANES), 1)
     first = jnp.bitwise_and(lane, 16) == 0
     high, low = iota((32, LANES), 0), iota((64, LANES), 0)
@@ -214,14 +224,11 @@
         hi_ref[...], lo_ref[...], (((1,), (1,)), ((), ())), preferred_element_type=F32
     )
     owned = jnp.concatenate([owned[0:16], owned[16:32]], 1)
-    words = words_ref[pl.ds(2 * lax.axis_index(FAR), 1), :]
-    place = iota((16, LANES), 0) * LANES + iota((16, LANES), 1)
-    slot = div30(place)
-    bit = jnp.bitwise_and(jnp.right_shift(lane_gather(words, slot), place - 30 * slot), 1)
-    owned_ref[...] = jnp.where(bit == 1, owned, 0.0)
+    owned_ref[...] = jnp.where(own_ref[...] == 1, owned, 0.0)
     cand = got_ref[4:12, :]
     for h in range(1, NFAR):
         cand = cand + got_ref[LAST * h + 4 : LAST * h + 12, :]
+    cand = cand * bits_ref[...]
     cand_ref[...] = cand
     total_ref[0, 0] = jnp.sum(cand)
 
@@ -269,16 +276,18 @@
         got0, near(tab), near(cand)
     )
     got1 = lax.all_to_all(give1.reshape(NNEAR, 1, 16 * LANES), NEAR, 0, 0, tiled=True)
+    own = call(ka_body, [VMEM], here((16, LANES), I32))(got0)
+    bits = call(kb_body, [VMEM], here((8, LANES), F32))(near(got1.reshape(NNEAR * 16, LANES)))
     give2 = call(k3_body, [VMEM], here((NFAR * LAST, LANES), F32))(near(got1.reshape(NNEAR * 16, LANES)))
     got2 = lax.all_to_all(give2.reshape(NFAR, 1, LAST * LANES), FAR, 0, 0, tiled=True)
     got2 = got2.reshape(NFAR * LAST, LANES)
     owned, cand, total = call(
         k4_body,
-        [VMEM, VMEM],
+        [VMEM, VMEM, VMEM],
         [shape((16, LANES), F32), shape((8, LANES), F32), shape((1, 1), F32)],
         [pltpu.VMEM((32, 64 * LANES), BF16), pltpu.VMEM((64, 64 * LANES), BF16)],
         [VMEM, VMEM, SMEM],
-    )(near(got2), got0)
+    )(near(got2), near(own), near(bits))
     return owned.reshape(SUP_DEV), cand.reshape(1024), total.reshape(())
 
 

time: 58.8 us -> 59.7 us (1.015)
  blocking collectives: 33.6 us -> 12.5 us
  waiting for transfers between devices: 3.92 us -> 15.7 us
  starting transfers between devices: 12.9 us -> 22.3 us
  Pallas kernels: 7.47 us -> 8.31 us
    all_to_all x1 -> x0, blocking collectives: 21.1 us -> none  [per_device(): lax.all_to_all(give2.reshape(NFAR, 1, LAST * LANES), FAR, 0, 0, tiled=True)]
    all_to_all x0 -> x1, waiting for transfers between devices: none -> 11.7 us  [per_device(): lax.all_to_all(give2.reshape(NFAR, 1, LAST * LANES), FAR, 0, 0, tiled=True)]
    all_to_all x0 -> x1, starting transfers between devices: none -> 9.38 us  [per_device(): lax.all_to_all(give2.reshape(NFAR, 1, LAST * LANES), FAR, 0, 0, tiled=True)]
    pallas_call x1, Pallas kernels: 0.18 us -> 0.84 us  [per_device(): call(k3_body, [VMEM], here((NFAR * LAST, LANES), F32))]
    pallas_call x1 -> x3, Pallas kernels: 1.43 us -> 1.6 us  [the longest x1 1.43 us: per_device(): call(k4_body, [VMEM, VMEM, VMEM], [shape((16, LANES), F32), shape((8, LAN...]
  transfers between devices with their start and end apart: 1 -> 2, of which waited for: 1 -> 2; matrix products, arithmetic and copies ran while one was open for 0% -> 0% of each run, Pallas kernels for 7% -> 7%
where the time goes in v5:
time: 59.7 us; the launch traced here: 59.4 us
  starting transfers between devices  22.3 us (37%)
  waiting for transfers between devices  15.7 us (26%)
  blocking collectives  12.5 us (21%)
  Pallas kernels  8.31 us (14%)
  between operations  0.66 us (1%)
    all_to_all x1, starting transfers between devices, per_device(): lax.all_to_all(give0.reshape(NCOL, 1, 2 * LANES), COL, 0, 0, tiled=True)  12.9 us
    all_to_all x1, blocking collectives, per_device(): lax.all_to_all(give1.reshape(NNEAR, 1, 16 * LANES), NEAR, 0, 0, tiled=True)  12.5 us
    all_to_all x1, waiting for transfers between devices, per_device(): lax.all_to_all(give2.reshape(NFAR, 1, LAST * LANES), FAR, 0, 0, tiled=True)  11.7 us
    all_to_all x1, starting transfers between devices, per_device(): lax.all_to_all(give2.reshape(NFAR, 1, LAST * LANES), FAR, 0, 0, tiled=True)  9.38 us
    pallas_call x1, Pallas kernels, per_device(): call(k1_body, [VMEM] * 5, [here((64, NDEV), F32), here((48, 1024), F32)],...  4.02 us
    all_to_all x1, waiting for transfers between devices, per_device(): lax.all_to_all(give0.reshape(NCOL, 1, 2 * LANES), COL, 0, 0, tiled=True)  3.92 us
    pallas_call x1, Pallas kernels, per_device(): call(k0_body, [VMEM, SMEM, VMEM], here((2 * NCOL, LANES), I32), [pltpu.VM...  1.58 us
    pallas_call x1, Pallas kernels, per_device(): call(k4_body, [VMEM, VMEM, VMEM], [shape((16, LANES), F32), shape((8, LAN...  1.43 us
  transfers between devices with their start and end apart: 2, of which 2 were waited for; matrix products, arithmetic and copies ran while one was open for 0% of the time, Pallas kernels for 7%

profile of v5, /device:TPU:1, one launch (start us, length us, event | category | flops | bytes accessed | tf_op | source)
XLA Modules:
  0.0 59.4 jit_solution(8973269008194037388)
XLA Ops:
  0.6 1.6 %k0_body.1 = s32[64,128]{1,0:T(8,128)} custom-call(s32[1104]{0:T(1024)} %words_ref.1, s32[3]{0:T(128)} %dates_ref.1, s32[8,128]{1,0:T(8,128)} %bitcast.21), custom_call_target="tpu_custom_call" | custom-call | tf_op jit(solution)/shard_map/k0_body/pallas_call | solution.py:258
  2.2 12.9 %all-to-all-start = ((s32[32,1,256]{2,1,0:T(1,128)}), s32[32,1,256]{2,1,0:T(1,128)S(1)}, u32[]{:S(2)}, u32[]{:S(2)}) async-start(s32[32,1,256]{2,1,0:T(1,128)} %bitcast.1), calls=%async_computation | async-start | bytes 65536 | tf_op jit(solution)/shard_map/all_to_all | solution.py:261
  15.1 4.0 %k1_body.1 = (f32[64,512]{1,0:T(8,128)S(1)}, f32[48,1024]{1,0:T(8,128)S(1)}) custom-call(s32[24,128]{1,0:T(8,128)} %bitcast.23, s32[24,128]{1,0:T(8,128)} %bitcast.24, s32[24,128]{1,0:T(8,128)} %bitcast.25, bf16[24,128]{1,0:T(8,128)(2,1)} %bitcast.26, s32[1,1024]{1,0:T(1,128)} %bitcast.22), custom_call_target="tpu_custom_call" | custom-call | tf_op jit(solution)/shard_map/k1_body/pallas_call | solution.py:263
  19.1 3.9 %all-to-all-done = s32[32,1,256]{2,1,0:T(1,128)S(1)} async-done(((s32[32,1,256]{2,1,0:T(1,128)}), s32[32,1,256]{2,1,0:T(1,128)S(1)}, u32[]{:S(2)}, u32[]{:S(2)}) %all-to-all-start) | async-done | bytes 32800 | tf_op jit(solution)/shard_map/all_to_all | solution.py:261
  23.0 0.3 k2_body.1
  23.3 12.5 %all_to_all.15 = f32[16,1,2048]{2,1,0:T(1,128)S(1)} all-to-all(f32[16,1,2048]{2,1,0:T(1,128)S(1)} %bitcast.18), channel_id=1, replica_groups=mesh['row_0'=2,'row_1'=8,'col_0'=2,'col_1'=8,'col_2'=2] {'col_1','col_2'}, dimensions={0} | all-to-all | bytes 262144 | tf_op jit(solution)/shard_map/all_to_all | solution.py:278
  35.8 0.8 %k3_body.1 = f32[384,128]{1,0:T(8,128)} custom-call(f32[256,128]{1,0:T(8,128)S(1)} %bitcast.15), custom_call_target="tpu_custom_call" | custom-call | tf_op jit(solution)/shard_map/k3_body/pallas_call | solution.py:281
  36.7 9.4 %all-to-all-start.2 = ((f32[32,1,1536]{2,1,0:T(1,128)}), f32[32,1,1536]{2,1,0:T(1,128)S(1)}, u32[]{:S(2)}, u32[]{:S(2)}) async-start(f32[32,1,1536]{2,1,0:T(1,128)} %bitcast.10), calls=%async_computation.2 | async-start | bytes 393216 | tf_op jit(solution)/shard_map/all_to_all | solution.py:282
  46.0 0.1 ka_body.1.own_ref
  46.1 0.1 kb_body.1.bits_ref
  46.2 11.7 %all-to-all-done.2 = f32[32,1,1536]{2,1,0:T(1,128)S(1)} async-done(((f32[32,1,1536]{2,1,0:T(1,128)}), f32[32,1,1536]{2,1,0:T(1,128)S(1)}, u32[]{:S(2)}, u32[]{:S(2)}) %all-to-all-start.2) | async-done | bytes 196640 | tf_op jit(solution)/shard_map/all_to_all | solution.py:282
  58.0 1.4 %k4_body.1 = (f32[16,128]{1,0:T(8,128)}, f32[8,128]{1,0:T(8,128)}, f32[1,1]{1,0:T(1,128)}) custom-call(f32[384,128]{1,0:T(8,128)S(1)} %bitcast.17, s32[16,128]{1,0:T(8,128)S(1)} %ka_body.1.own_ref, f32[8,128]{1,0:T(8,128)S(1)} %kb_body.1.bits_ref), custom_call_target="tpu_custom_call" | custom-call | tf_op jit(solution)/shard_map/k4_body/pallas_call | solution.py:284
Async XLA Ops:
  2.2 20.8 %all-to-all-start = ((s32[32,1,256]{2,1,0:T(1,128)}), s32[32,1,256]{2,1,0:T(1,128)S(1)}, u32[]{:S(2)}, u32[]{:S(2)}) async-start(s32[32,1,256]{2,1,0:T(1,128)} %bitcast.1), calls=%async_computation | async-start | bytes 65536 | tf_op jit(solution)/shard_map/all_to_all | solution.py:261
  36.7 21.3 %all-to-all-start.2 = ((f32[32,1,1536]{2,1,0:T(1,128)}), f32[32,1,1536]{2,1,0:T(1,128)S(1)}, u32[]{:S(2)}, u32[]{:S(2)}) async-start(f32[32,1,1536]{2,1,0:T(1,128)} %bitcast.10), calls=%async_computation.2 | async-start | bytes 393216 | tf_op jit(solution)/shard_map/all_to_all | solution.py:282

commit v6 on v4

--- a/solution.py
+++ b/solution.py
@@ -13,6 +13,7 @@
 ROW_COL = ROW + COL
 NEAR = ("col_1", "col_2")
 FAR = ("row_0", "row_1", "col_0")
+FAR_SENT = ("row_1", "row_0", "col_0")
 
 NNEAR, NFAR, NCOL, NDEV = 16, 32, 32, 512
 SUP_DEV = 2048
@@ -190,7 +191,8 @@
             tile = roll(rows[0], -32 * lo)
             for q in range(1, 4):
                 tile = jnp.where(jnp.right_shift(lane, 5) == q, roll(rows[q], 32 * (q - lo)), tile)
-            at = LAST * (4 * hi + lo)
+            to = 4 * hi + lo
+            at = LAST * (4 * (to // 2 % 8) + 2 * (to // 16) + to % 2)
             out_ref[at : at + 4, :] = jnp.where(jnp.bitwise_and(lane, 15) < 12, tile, 0.0)
             out_ref[at + 4 : at + 12, :] = total
 
@@ -270,7 +272,7 @@
     )
     got1 = lax.all_to_all(give1.reshape(NNEAR, 1, 16 * LANES), NEAR, 0, 0, tiled=True)
     give2 = call(k3_body, [VMEM], here((NFAR * LAST, LANES), F32))(near(got1.reshape(NNEAR * 16, LANES)))
-    got2 = lax.all_to_all(give2.reshape(NFAR, 1, LAST * LANES), FAR, 0, 0, tiled=True)
+    got2 = lax.all_to_all(give2.reshape(NFAR, 1, LAST * LANES), FAR_SENT, 0, 0, tiled=True)
     got2 = got2.reshape(NFAR * LAST, LANES)
     owned, cand, total = call(
         k4_body,

time: 58.8 us -> 58 us (0.986)
  blocking collectives: 33.6 us -> 32.8 us
    all_to_all x1, blocking collectives: 21.1 us -> 20.3 us  [per_device(): lax.all_to_all(give2.reshape(NFAR, 1, LAST * LANES), FAR_SENT, 0, 0, tile...]
where the time goes in v6:
time: 58 us; the launch traced here: 57.7 us
  blocking collectives  32.8 us (57%)
  starting transfers between devices  12.9 us (22%)
  Pallas kernels  7.48 us (13%)
  waiting for transfers between devices  3.92 us (7%)
  between operations  0.66 us (1%)
    all_to_all x1, blocking collectives, per_device(): lax.all_to_all(give2.reshape(NFAR, 1, LAST * LANES), FAR_SENT, 0, 0, tile...  20.3 us
    all_to_all x1, starting transfers between devices, per_device(): lax.all_to_all(give0.reshape(NCOL, 1, 2 * LANES), COL, 0, 0, tiled=True)  12.9 us
    all_to_all x1, blocking collectives, per_device(): lax.all_to_all(give1.reshape(NNEAR, 1, 16 * LANES), NEAR, 0, 0, tiled=True)  12.5 us
    pallas_call x1, Pallas kernels, per_device(): call(k1_body, [VMEM] * 5, [here((64, NDEV), F32), here((48, 1024), F32)],...  4.02 us
    all_to_all x1, waiting for transfers between devices, per_device(): lax.all_to_all(give0.reshape(NCOL, 1, 2 * LANES), COL, 0, 0, tiled=True)  3.92 us
    pallas_call x1, Pallas kernels, per_device(): call(k0_body, [VMEM, SMEM, VMEM], here((2 * NCOL, LANES), I32), [pltpu.VM...  1.57 us
    pallas_call x1, Pallas kernels, per_device(): call(k4_body, [VMEM, VMEM], [shape((16, LANES), F32), shape((8, LANES), F...  1.43 us
  transfers between devices with their start and end apart: 1, of which 1 were waited for; matrix products, arithmetic and copies ran while one was open for 0% of the time, Pallas kernels for 7%

profile of v6, /device:TPU:1, one launch (start us, length us, event | category | flops | bytes accessed | tf_op | source)
XLA Modules:
  0.0 57.7 jit_solution(17164633885511093177)
XLA Ops:
  0.6 1.6 %k0_body.1 = s32[64,128]{1,0:T(8,128)} custom-call(s32[1104]{0:T(1024)} %words_ref.1, s32[3]{0:T(128)} %dates_ref.1, s32[8,128]{1,0:T(8,128)} %bitcast.21), custom_call_target="tpu_custom_call" | custom-call | tf_op jit(solution)/shard_map/k0_body/pallas_call | solution.py:253
  2.2 12.9 %all-to-all-start = ((s32[32,1,256]{2,1,0:T(1,128)}), s32[32,1,256]{2,1,0:T(1,128)S(1)}, u32[]{:S(2)}, u32[]{:S(2)}) async-start(s32[32,1,256]{2,1,0:T(1,128)} %bitcast.1), calls=%async_computation | async-start | bytes 65536 | tf_op jit(solution)/shard_map/all_to_all | solution.py:256
  15.1 4.0 %k1_body.1 = (f32[64,512]{1,0:T(8,128)S(1)}, f32[48,1024]{1,0:T(8,128)S(1)}) custom-call(s32[24,128]{1,0:T(8,128)} %bitcast.23, s32[24,128]{1,0:T(8,128)} %bitcast.24, s32[24,128]{1,0:T(8,128)} %bitcast.25, bf16[24,128]{1,0:T(8,128)(2,1)} %bitcast.26, s32[1,1024]{1,0:T(1,128)} %bitcast.22), custom_call_target="tpu_custom_call" | custom-call | tf_op jit(solution)/shard_map/k1_body/pallas_call | solution.py:258
  19.1 3.9 %all-to-all-done = s32[32,1,256]{2,1,0:T(1,128)S(1)} async-done(((s32[32,1,256]{2,1,0:T(1,128)}), s32[32,1,256]{2,1,0:T(1,128)S(1)}, u32[]{:S(2)}, u32[]{:S(2)}) %all-to-all-start) | async-done | bytes 32800 | tf_op jit(solution)/shard_map/all_to_all | solution.py:256
  23.0 0.3 k2_body.1
  23.3 12.5 %all_to_all.15 = f32[16,1,2048]{2,1,0:T(1,128)S(1)} all-to-all(f32[16,1,2048]{2,1,0:T(1,128)S(1)} %bitcast.18), channel_id=1, replica_groups=mesh['row_0'=2,'row_1'=8,'col_0'=2,'col_1'=8,'col_2'=2] {'col_1','col_2'}, dimensions={0} | all-to-all | bytes 262144 | tf_op jit(solution)/shard_map/all_to_all | solution.py:273
  35.8 0.2 k3_body.1
  36.0 20.3 %all_to_all.16 = f32[32,1,1536]{2,1,0:T(1,128)S(1)} all-to-all(f32[32,1,1536]{2,1,0:T(1,128)S(1)} %bitcast.16), channel_id=1, replica_groups=mesh['row_0'=2,'row_1'=8,'col_0'=2,'col_1'=8,'col_2'=2] {'row_1','row_0'..., dimensions={0} | all-to-all | bytes 393216 | tf_op jit(solution)/shard_map/all_to_all | solution.py:275
  56.3 1.4 %k4_body.1 = (f32[16,128]{1,0:T(8,128)}, f32[8,128]{1,0:T(8,128)}, f32[1,1]{1,0:T(1,128)}) custom-call(f32[384,128]{1,0:T(8,128)S(1)} %bitcast.15, s32[64,128]{1,0:T(8,128)S(1)} %bitcast.20), custom_call_target="tpu_custom_call" | custom-call | tf_op jit(solution)/shard_map/k4_body/pallas_call | solution.py:277
Async XLA Ops:
  2.2 20.8 %all-to-all-start = ((s32[32,1,256]{2,1,0:T(1,128)}), s32[32,1,256]{2,1,0:T(1,128)S(1)}, u32[]{:S(2)}, u32[]{:S(2)}) async-start(s32[32,1,256]{2,1,0:T(1,128)} %bitcast.1), calls=%async_computation | async-start | bytes 65536 | tf_op jit(solution)/shard_map/all_to_all | solution.py:256

commit v7 on v6

--- a/solution.py
+++ b/solution.py
@@ -8,12 +8,12 @@
 from jax.sharding import Mesh
 from jax.sharding import PartitionSpec as P
 
-ROW = ("row_0", "row_1")
-COL = ("col_0", "col_1", "col_2")
-ROW_COL = ROW + COL
-NEAR = ("col_1", "col_2")
-FAR = ("row_0", "row_1", "col_0")
-FAR_SENT = ("row_1", "row_0", "col_0")
+XH, Y2, Y1, Y0, XL, Z2, Z1, Z0, CORE = AXES = ("xh", "y2", "y1", "y0", "xl", "z2", "z1", "z0", "core")
+COL = (XL, Z2, Z1, Z0, CORE)
+NEAR = (Z2, Z1, Z0, CORE)
+FAR = (XH, Y2, Y1, Y0, XL)
+COL_SENT = (Z2, Z1, Z0, CORE, XL)
+FAR_SENT = (Y0, Y1, Y2, XL, XH)
 
 NNEAR, NFAR, NCOL, NDEV = 16, 32, 32, 512
 SUP_DEV = 2048
@@ -51,7 +51,7 @@
     return out
 
 
-def k0_body(words_ref, dates_ref, cands_ref, out_ref, bits_ref):
+def k0_body(words_ref, dates_ref, cands_ref, out_ref):
     col = lax.axis_index(COL)
     words = [words_ref[i * LANES : (i + 1) * LANES].reshape(1, LANES) for i in range(8)]
     last = words_ref[8 * LANES : 16 * WORDS].reshape(1, 16 * WORDS - 8 * LANES)
@@ -63,17 +63,16 @@
     slot = div30(off)
     word = lookup(words, jnp.where(mine, block * WORDS + slot, 0))
     bits = jnp.where(mine, jnp.bitwise_and(jnp.right_shift(word, off - 30 * slot), 1), 0)
-    bits_ref[0:8, :] = bits
-    bits_ref[8:16, :] = bits
     sub, lane = iota((8, LANES), 0), iota((8, LANES), 1)
-    for j in range(4):
-        m = jnp.bitwise_and(4 * sub + j, 15)
+    for i in range(2):
+        m = 2 * sub + i
         own = lookup(words, jnp.where(lane < WORDS, m * WORDS + lane, 0))
         row = jnp.where(lane < WORDS, own, 0)
         for d in range(3):
             row = jnp.where(lane == DATES_AT + d, dates_ref[d], row)
-        out_ref[pl.ds(2 * j, 8, stride=8), :] = row
-        out_ref[pl.ds(2 * j + 1, 8, stride=8), :] = roll(bits_ref[pl.ds(j // 2, 8, stride=2), :], 64 * (j % 2))
+        for j in (4 * i, 4 * i + 2):
+            out_ref[pl.ds(j, 8, stride=8), :] = row
+            out_ref[pl.ds(j + 1, 8, stride=8), :] = roll(bits, 64 * i)
 
 
 def k1_body(block_ref, off_ref, date_ref, rev_ref, cands_ref, tab_ref, cand_ref, hot_ref, val_ref):
@@ -137,6 +136,7 @@
 def k2_body(got_ref, tab_ref, cand_ref, out_ref, tmp_ref):
     got = got_ref[pl.ds(0, NCOL, stride=2), :]
     src, lane = iota((NCOL, LANES), 0), iota((NCOL, LANES), 1)
+    src = 16 * jnp.bitwise_and(src, 1) + jnp.right_shift(src, 1)
     table = jnp.zeros((NCOL, LANES), I32)
     for j in range(3):
         word = jnp.broadcast_to(got[:, DATES_AT + j : DATES_AT + j + 1], (NCOL, LANES))
@@ -192,7 +192,7 @@
             for q in range(1, 4):
                 tile = jnp.where(jnp.right_shift(lane, 5) == q, roll(rows[q], 32 * (q - lo)), tile)
             to = 4 * hi + lo
-            at = LAST * (4 * (to // 2 % 8) + 2 * (to // 16) + to % 2)
+            at = LAST * sum((to >> b & 1) << p for b, p in ((4, 0), (3, 2), (2, 3), (1, 4), (0, 1)))
             out_ref[at : at + 4, :] = jnp.where(jnp.bitwise_and(lane, 15) < 12, tile, 0.0)
             out_ref[at + 4 : at + 12, :] = total
 
@@ -216,7 +216,8 @@
         hi_ref[...], lo_ref[...], (((1,), (1,)), ((), ())), preferred_element_type=F32
     )
     owned = jnp.concatenate([owned[0:16], owned[16:32]], 1)
-    words = words_ref[pl.ds(2 * lax.axis_index(FAR), 1), :]
+    far = lax.axis_index(FAR)
+    words = words_ref[pl.ds(4 * jnp.bitwise_and(far, 15) + 2 * jnp.right_shift(far, 4), 1), :]
     place = iota((16, LANES), 0) * LANES + iota((16, LANES), 1)
     slot = div30(place)
     bit = jnp.bitwise_and(jnp.right_shift(lane_gather(words, slot), place - 30 * slot), 1)
@@ -225,7 +226,7 @@
     for h in range(1, NFAR):
         cand = cand + got_ref[LAST * h + 4 : LAST * h + 12, :]
     cand_ref[...] = cand
-    total_ref[0, 0] = jnp.sum(cand)
+    total_ref[...] = jnp.sum(jnp.sum(cand, axis=0, keepdims=True), axis=1, keepdims=True)
 
 
 SMEM = pl.BlockSpec(memory_space=pltpu.SMEM)
@@ -250,10 +251,10 @@
 
 def per_device(fact_block, fact_offset, fact_date, revenue, supplier_words, date_words, candidates):
     cands = candidates.reshape(8, LANES)
-    give0 = call(k0_body, [VMEM, SMEM, VMEM], here((2 * NCOL, LANES), I32), [pltpu.VMEM((16, LANES), I32)])(
+    give0 = call(k0_body, [VMEM, SMEM, VMEM], here((2 * NCOL, LANES), I32))(
         supplier_words, date_words, cands
     )
-    got0 = lax.all_to_all(give0.reshape(NCOL, 1, 2 * LANES), COL, 0, 0, tiled=True)
+    got0 = lax.all_to_all(give0.reshape(NCOL, 1, 2 * LANES), COL_SENT, 0, 0, tiled=True)
     got0 = near(got0.reshape(2 * NCOL, LANES))
     tab, cand = call(
         k1_body,
@@ -279,17 +280,16 @@
         [VMEM, VMEM],
         [shape((16, LANES), F32), shape((8, LANES), F32), shape((1, 1), F32)],
         [pltpu.VMEM((32, 64 * LANES), BF16), pltpu.VMEM((64, 64 * LANES), BF16)],
-        [VMEM, VMEM, SMEM],
     )(near(got2), got0)
     return owned.reshape(SUP_DEV), cand.reshape(1024), total.reshape(())
 
 
 def solution(mesh):
-    split = Mesh(mesh.devices.reshape(2, 8, 2, 8, 2), ROW_COL)
+    split = Mesh(mesh.devices.reshape((2,) * 9), AXES)
     return jax.shard_map(
         per_device,
         mesh=split,
-        in_specs=(P(ROW_COL, None), P(ROW_COL), P(ROW_COL), P(ROW_COL), P(COL), P(COL), P()),
-        out_specs=(P(ROW_COL), P(), P()),
+        in_specs=(P(AXES, None), P(AXES), P(AXES), P(AXES), P(COL), P(COL), P()),
+        out_specs=(P(AXES), P(), P()),
         check_vma=False,
     )

time: 58 us -> 57 us (0.983)
  blocking collectives: 32.8 us -> 31.8 us
    all_to_all x1, blocking collectives: 20.3 us -> 19.4 us  [per_device(): lax.all_to_all(give2.reshape(NFAR, 1, LAST * LANES), FAR_SENT, 0, 0, tile...]
where the time goes in v7:
time: 57 us; the launch traced here: 56.7 us
  blocking collectives  31.8 us (56%)
  starting transfers between devices  12.9 us (23%)
  Pallas kernels  7.47 us (13%)
  waiting for transfers between devices  3.88 us (7%)
  between operations  0.66 us (1%)
    all_to_all x1, blocking collectives, per_device(): lax.all_to_all(give2.reshape(NFAR, 1, LAST * LANES), FAR_SENT, 0, 0, tile...  19.4 us
    all_to_all x1, starting transfers between devices, per_device(): lax.all_to_all(give0.reshape(NCOL, 1, 2 * LANES), COL_SENT, 0, 0, tiled=T...  12.9 us
    all_to_all x1, blocking collectives, per_device(): lax.all_to_all(give1.reshape(NNEAR, 1, 16 * LANES), NEAR, 0, 0, tiled=True)  12.3 us
    pallas_call x1, Pallas kernels, per_device(): call(k1_body, [VMEM] * 5, [here((64, NDEV), F32), here((48, 1024), F32)],...  4.02 us
    all_to_all x1, waiting for transfers between devices, per_device(): lax.all_to_all(give0.reshape(NCOL, 1, 2 * LANES), COL_SENT, 0, 0, tiled=T...  3.88 us
    pallas_call x1, Pallas kernels, per_device(): call(k0_body, [VMEM, SMEM, VMEM], here((2 * NCOL, LANES), I32))  1.57 us
    pallas_call x1, Pallas kernels, per_device(): call(k4_body, [VMEM, VMEM], [shape((16, LANES), F32), shape((8, LANES), F...  1.42 us
  transfers between devices with their start and end apart: 1, of which 1 were waited for; matrix products, arithmetic and copies ran while one was open for 0% of the time, Pallas kernels for 7%

profile of v7, /device:TPU:1, one launch (start us, length us, event | category | flops | bytes accessed | tf_op | source)
XLA Modules:
  0.0 56.7 jit_solution(15961581603994836218)
XLA Ops:
  0.6 1.6 %k0_body.1 = s32[64,128]{1,0:T(8,128)} custom-call(s32[1104]{0:T(1024)} %words_ref.1, s32[3]{0:T(128)} %dates_ref.1, s32[8,128]{1,0:T(8,128)} %bitcast.21), custom_call_target="tpu_custom_call" | custom-call | tf_op jit(solution)/shard_map/k0_body/pallas_call | solution.py:254
  2.2 12.9 %all-to-all-start = ((s32[32,1,256]{2,1,0:T(1,128)}), s32[32,1,256]{2,1,0:T(1,128)S(1)}, u32[]{:S(2)}, u32[]{:S(2)}) async-start(s32[32,1,256]{2,1,0:T(1,128)} %bitcast.1), calls=%async_computation | async-start | bytes 65536 | tf_op jit(solution)/shard_map/all_to_all | solution.py:257
  15.1 4.0 %k1_body.1 = (f32[64,512]{1,0:T(8,128)S(1)}, f32[48,1024]{1,0:T(8,128)S(1)}) custom-call(s32[24,128]{1,0:T(8,128)} %bitcast.23, s32[24,128]{1,0:T(8,128)} %bitcast.24, s32[24,128]{1,0:T(8,128)} %bitcast.25, bf16[24,128]{1,0:T(8,128)(2,1)} %bitcast.26, s32[1,1024]{1,0:T(1,128)} %bitcast.22), custom_call_target="tpu_custom_call" | custom-call | tf_op jit(solution)/shard_map/k1_body/pallas_call | solution.py:259
  19.1 3.9 %all-to-all-done = s32[32,1,256]{2,1,0:T(1,128)S(1)} async-done(((s32[32,1,256]{2,1,0:T(1,128)}), s32[32,1,256]{2,1,0:T(1,128)S(1)}, u32[]{:S(2)}, u32[]{:S(2)}) %all-to-all-start) | async-done | bytes 32800 | tf_op jit(solution)/shard_map/all_to_all | solution.py:257
  23.0 0.3 k2_body.1
  23.3 12.3 %all_to_all.15 = f32[16,1,2048]{2,1,0:T(1,128)S(1)} all-to-all(f32[16,1,2048]{2,1,0:T(1,128)S(1)} %bitcast.18), channel_id=1, replica_groups=mesh['xh'=2,'y2'=2,'y1'=2,'y0'=2,'xl'=2,'z2'=2,'z1'=2,'z0'=2,'core'=2] {..., dimensions={0} | all-to-all | bytes 262144 | tf_op jit(solution)/shard_map/all_to_all | solution.py:274
  35.6 0.2 k3_body.1
  35.8 19.4 %all_to_all.16 = f32[32,1,1536]{2,1,0:T(1,128)S(1)} all-to-all(f32[32,1,1536]{2,1,0:T(1,128)S(1)} %bitcast.16), channel_id=1, replica_groups=mesh['xh'=2,'y2'=2,'y1'=2,'y0'=2,'xl'=2,'z2'=2,'z1'=2,'z0'=2,'core'=2] {..., dimensions={0} | all-to-all | bytes 393216 | tf_op jit(solution)/shard_map/all_to_all | solution.py:276
  55.3 1.4 %k4_body.1 = (f32[16,128]{1,0:T(8,128)}, f32[8,128]{1,0:T(8,128)}, f32[1,1]{1,0:T(1,128)}) custom-call(f32[384,128]{1,0:T(8,128)S(1)} %bitcast.15, s32[64,128]{1,0:T(8,128)S(1)} %bitcast.20), custom_call_target="tpu_custom_call" | custom-call | tf_op jit(solution)/shard_map/k4_body/pallas_call | solution.py:278
Async XLA Ops:
  2.2 20.8 %all-to-all-start = ((s32[32,1,256]{2,1,0:T(1,128)}), s32[32,1,256]{2,1,0:T(1,128)S(1)}, u32[]{:S(2)}, u32[]{:S(2)}) async-start(s32[32,1,256]{2,1,0:T(1,128)} %bitcast.1), calls=%async_computation | async-start | bytes 65536 | tf_op jit(solution)/shard_map/all_to_all | solution.py:257

commit v8 on v7

--- a/solution.py
+++ b/solution.py
@@ -13,7 +13,7 @@
 NEAR = (Z2, Z1, Z0, CORE)
 FAR = (XH, Y2, Y1, Y0, XL)
 COL_SENT = (Z2, Z1, Z0, CORE, XL)
-FAR_SENT = (Y0, Y1, Y2, XL, XH)
+FAR_SENT = (Y0, Y2, Y1, XL, XH)
 
 NNEAR, NFAR, NCOL, NDEV = 16, 32, 32, 512
 SUP_DEV = 2048
@@ -64,12 +64,12 @@
     word = lookup(words, jnp.where(mine, block * WORDS + slot, 0))
     bits = jnp.where(mine, jnp.bitwise_and(jnp.right_shift(word, off - 30 * slot), 1), 0)
     sub, lane = iota((8, LANES), 0), iota((8, LANES), 1)
+    dates = jnp.concatenate([dates_ref[...].reshape(1, 3), jnp.zeros((1, LANES - 3), I32)], 1)
+    dates = roll(jnp.broadcast_to(dates, (8, LANES)), DATES_AT)
     for i in range(2):
         m = 2 * sub + i
         own = lookup(words, jnp.where(lane < WORDS, m * WORDS + lane, 0))
-        row = jnp.where(lane < WORDS, own, 0)
-        for d in range(3):
-            row = jnp.where(lane == DATES_AT + d, dates_ref[d], row)
+        row = jnp.where(lane < WORDS, own, dates)
         for j in (4 * i, 4 * i + 2):
             out_ref[pl.ds(j, 8, stride=8), :] = row
             out_ref[pl.ds(j + 1, 8, stride=8), :] = roll(bits, 64 * i)
@@ -192,7 +192,7 @@
             for q in range(1, 4):
                 tile = jnp.where(jnp.right_shift(lane, 5) == q, roll(rows[q], 32 * (q - lo)), tile)
             to = 4 * hi + lo
-            at = LAST * sum((to >> b & 1) << p for b, p in ((4, 0), (3, 2), (2, 3), (1, 4), (0, 1)))
+            at = LAST * sum((to >> b & 1) << p for b, p in ((4, 0), (3, 3), (2, 2), (1, 4), (0, 1)))
             out_ref[at : at + 4, :] = jnp.where(jnp.bitwise_and(lane, 15) < 12, tile, 0.0)
             out_ref[at + 4 : at + 12, :] = total
 
@@ -251,7 +251,7 @@
 
 def per_device(fact_block, fact_offset, fact_date, revenue, supplier_words, date_words, candidates):
     cands = candidates.reshape(8, LANES)
-    give0 = call(k0_body, [VMEM, SMEM, VMEM], here((2 * NCOL, LANES), I32))(
+    give0 = call(k0_body, [VMEM, VMEM, VMEM], here((2 * NCOL, LANES), I32))(
         supplier_words, date_words, cands
     )
     got0 = lax.all_to_all(give0.reshape(NCOL, 1, 2 * LANES), COL_SENT, 0, 0, tiled=True)

time: 57 us -> 58.2 us (1.021)
  blocking collectives: 31.8 us -> 33.1 us
    all_to_all x1, blocking collectives: 19.4 us -> 20.8 us  [per_device(): lax.all_to_all(give2.reshape(NFAR, 1, LAST * LANES), FAR_SENT, 0, 0, tile...]
where the time goes in v8:
time: 58.2 us; the launch traced here: 57.9 us
  blocking collectives  33.1 us (57%)
  starting transfers between devices  12.9 us (22%)
  Pallas kernels  7.38 us (13%)
  waiting for transfers between devices  3.88 us (7%)
  between operations  0.66 us (1%)
    all_to_all x1, blocking collectives, per_device(): lax.all_to_all(give2.reshape(NFAR, 1, LAST * LANES), FAR_SENT, 0, 0, tile...  20.8 us
    all_to_all x1, starting transfers between devices, per_device(): lax.all_to_all(give0.reshape(NCOL, 1, 2 * LANES), COL_SENT, 0, 0, tiled=T...  12.9 us
    all_to_all x1, blocking collectives, per_device(): lax.all_to_all(give1.reshape(NNEAR, 1, 16 * LANES), NEAR, 0, 0, tiled=True)  12.3 us
    pallas_call x1, Pallas kernels, per_device(): call(k1_body, [VMEM] * 5, [here((64, NDEV), F32), here((48, 1024), F32)],...  4.02 us
    all_to_all x1, waiting for transfers between devices, per_device(): lax.all_to_all(give0.reshape(NCOL, 1, 2 * LANES), COL_SENT, 0, 0, tiled=T...  3.88 us
    pallas_call x1, Pallas kernels, per_device(): call(k0_body, [VMEM, VMEM, VMEM], here((2 * NCOL, LANES), I32))  1.49 us
    pallas_call x1, Pallas kernels, per_device(): call(k4_body, [VMEM, VMEM], [shape((16, LANES), F32), shape((8, LANES), F...  1.42 us
  transfers between devices with their start and end apart: 1, of which 1 were waited for; matrix products, arithmetic and copies ran while one was open for 0% of the time, Pallas kernels for 7%

profile of v8, /device:TPU:1, one launch (start us, length us, event | category | flops | bytes accessed | tf_op | source)
XLA Modules:
  0.0 57.9 jit_solution(1831210969045689588)
XLA Ops:
  0.6 1.5 %k0_body.1 = s32[64,128]{1,0:T(8,128)} custom-call(s32[1104]{0:T(1024)} %words_ref.1, s32[3]{0:T(128)} %dates_ref.1, s32[8,128]{1,0:T(8,128)} %bitcast.21), custom_call_target="tpu_custom_call" | custom-call | tf_op jit(solution)/shard_map/k0_body/pallas_call | solution.py:254
  2.1 12.9 %all-to-all-start = ((s32[32,1,256]{2,1,0:T(1,128)}), s32[32,1,256]{2,1,0:T(1,128)S(1)}, u32[]{:S(2)}, u32[]{:S(2)}) async-start(s32[32,1,256]{2,1,0:T(1,128)} %bitcast.1), calls=%async_computation | async-start | bytes 65536 | tf_op jit(solution)/shard_map/all_to_all | solution.py:257
  15.0 4.0 %k1_body.1 = (f32[64,512]{1,0:T(8,128)S(1)}, f32[48,1024]{1,0:T(8,128)S(1)}) custom-call(s32[24,128]{1,0:T(8,128)} %bitcast.23, s32[24,128]{1,0:T(8,128)} %bitcast.24, s32[24,128]{1,0:T(8,128)} %bitcast.25, bf16[24,128]{1,0:T(8,128)(2,1)} %bitcast.26, s32[1,1024]{1,0:T(1,128)} %bitcast.22), custom_call_target="tpu_custom_call" | custom-call | tf_op jit(solution)/shard_map/k1_body/pallas_call | solution.py:259
  19.0 3.9 %all-to-all-done = s32[32,1,256]{2,1,0:T(1,128)S(1)} async-done(((s32[32,1,256]{2,1,0:T(1,128)}), s32[32,1,256]{2,1,0:T(1,128)S(1)}, u32[]{:S(2)}, u32[]{:S(2)}) %all-to-all-start) | async-done | bytes 32800 | tf_op jit(solution)/shard_map/all_to_all | solution.py:257
  22.9 0.3 k2_body.1
  23.2 12.3 %all_to_all.15 = f32[16,1,2048]{2,1,0:T(1,128)S(1)} all-to-all(f32[16,1,2048]{2,1,0:T(1,128)S(1)} %bitcast.18), channel_id=1, replica_groups=mesh['xh'=2,'y2'=2,'y1'=2,'y0'=2,'xl'=2,'z2'=2,'z1'=2,'z0'=2,'core'=2] {..., dimensions={0} | all-to-all | bytes 262144 | tf_op jit(solution)/shard_map/all_to_all | solution.py:274
  35.5 0.2 k3_body.1
  35.7 20.8 %all_to_all.16 = f32[32,1,1536]{2,1,0:T(1,128)S(1)} all-to-all(f32[32,1,1536]{2,1,0:T(1,128)S(1)} %bitcast.16), channel_id=1, replica_groups=mesh['xh'=2,'y2'=2,'y1'=2,'y0'=2,'xl'=2,'z2'=2,'z1'=2,'z0'=2,'core'=2] {..., dimensions={0} | all-to-all | bytes 393216 | tf_op jit(solution)/shard_map/all_to_all | solution.py:276
  56.5 1.4 %k4_body.1 = (f32[16,128]{1,0:T(8,128)}, f32[8,128]{1,0:T(8,128)}, f32[1,1]{1,0:T(1,128)}) custom-call(f32[384,128]{1,0:T(8,128)S(1)} %bitcast.15, s32[64,128]{1,0:T(8,128)S(1)} %bitcast.20), custom_call_target="tpu_custom_call" | custom-call | tf_op jit(solution)/shard_map/k4_body/pallas_call | solution.py:278
Async XLA Ops:
  2.1 20.8 %all-to-all-start = ((s32[32,1,256]{2,1,0:T(1,128)}), s32[32,1,256]{2,1,0:T(1,128)S(1)}, u32[]{:S(2)}, u32[]{:S(2)}) async-start(s32[32,1,256]{2,1,0:T(1,128)} %bitcast.1), calls=%async_computation | async-start | bytes 65536 | tf_op jit(solution)/shard_map/all_to_all | solution.py:257

commit v9 on v8

--- a/solution.py
+++ b/solution.py
@@ -13,7 +13,7 @@
 NEAR = (Z2, Z1, Z0, CORE)
 FAR = (XH, Y2, Y1, Y0, XL)
 COL_SENT = (Z2, Z1, Z0, CORE, XL)
-FAR_SENT = (Y0, Y2, Y1, XL, XH)
+FAR_SENT = (Y0, Y1, XL, XH, Y2)
 
 NNEAR, NFAR, NCOL, NDEV = 16, 32, 32, 512
 SUP_DEV = 2048
@@ -192,7 +192,7 @@
             for q in range(1, 4):
                 tile = jnp.where(jnp.right_shift(lane, 5) == q, roll(rows[q], 32 * (q - lo)), tile)
             to = 4 * hi + lo
-            at = LAST * sum((to >> b & 1) << p for b, p in ((4, 0), (3, 3), (2, 2), (1, 4), (0, 1)))
+            at = LAST * sum((to >> b & 1) << p for b, p in ((4, 1), (3, 0), (2, 3), (1, 4), (0, 2)))
             out_ref[at : at + 4, :] = jnp.where(jnp.bitwise_and(lane, 15) < 12, tile, 0.0)
             out_ref[at + 4 : at + 12, :] = total
 

time: 58.2 us -> 57.4 us (0.986)
  blocking collectives: 33.1 us -> 31.9 us
    all_to_all x1, blocking collectives: 20.8 us -> 19.6 us  [per_device(): lax.all_to_all(give2.reshape(NFAR, 1, LAST * LANES), FAR_SENT, 0, 0, tile...]
where the time goes in v9:
time: 57.4 us; the launch traced here: 56.7 us
  blocking collectives  31.9 us (56%)
  starting transfers between devices  12.9 us (22%)
  Pallas kernels  7.38 us (13%)
  waiting for transfers between devices  3.88 us (7%)
  between operations  0.66 us (1%)
    all_to_all x1, blocking collectives, per_device(): lax.all_to_all(give2.reshape(NFAR, 1, LAST * LANES), FAR_SENT, 0, 0, tile...  19.6 us
    all_to_all x1, starting transfers between devices, per_device(): lax.all_to_all(give0.reshape(NCOL, 1, 2 * LANES), COL_SENT, 0, 0, tiled=T...  12.9 us
    all_to_all x1, blocking collectives, per_device(): lax.all_to_all(give1.reshape(NNEAR, 1, 16 * LANES), NEAR, 0, 0, tiled=True)  12.3 us
    pallas_call x1, Pallas kernels, per_device(): call(k1_body, [VMEM] * 5, [here((64, NDEV), F32), here((48, 1024), F32)],...  4.02 us
    all_to_all x1, waiting for transfers between devices, per_device(): lax.all_to_all(give0.reshape(NCOL, 1, 2 * LANES), COL_SENT, 0, 0, tiled=T...  3.88 us
    pallas_call x1, Pallas kernels, per_device(): call(k0_body, [VMEM, VMEM, VMEM], here((2 * NCOL, LANES), I32))  1.49 us
    pallas_call x1, Pallas kernels, per_device(): call(k4_body, [VMEM, VMEM], [shape((16, LANES), F32), shape((8, LANES), F...  1.42 us
  transfers between devices with their start and end apart: 1, of which 1 were waited for; matrix products, arithmetic and copies ran while one was open for 0% of the time, Pallas kernels for 7%

profile of v9, /device:TPU:1, one launch (start us, length us, event | category | flops | bytes accessed | tf_op | source)
XLA Modules:
  0.0 56.7 jit_solution(10483274279179065629)
XLA Ops:
  0.6 1.5 %k0_body.1 = s32[64,128]{1,0:T(8,128)} custom-call(s32[1104]{0:T(1024)} %words_ref.1, s32[3]{0:T(128)} %dates_ref.1, s32[8,128]{1,0:T(8,128)} %bitcast.21), custom_call_target="tpu_custom_call" | custom-call | tf_op jit(solution)/shard_map/k0_body/pallas_call | solution.py:254
  2.1 12.9 %all-to-all-start = ((s32[32,1,256]{2,1,0:T(1,128)}), s32[32,1,256]{2,1,0:T(1,128)S(1)}, u32[]{:S(2)}, u32[]{:S(2)}) async-start(s32[32,1,256]{2,1,0:T(1,128)} %bitcast.1), calls=%async_computation | async-start | bytes 65536 | tf_op jit(solution)/shard_map/all_to_all | solution.py:257
  15.0 4.0 %k1_body.1 = (f32[64,512]{1,0:T(8,128)S(1)}, f32[48,1024]{1,0:T(8,128)S(1)}) custom-call(s32[24,128]{1,0:T(8,128)} %bitcast.23, s32[24,128]{1,0:T(8,128)} %bitcast.24, s32[24,128]{1,0:T(8,128)} %bitcast.25, bf16[24,128]{1,0:T(8,128)(2,1)} %bitcast.26, s32[1,1024]{1,0:T(1,128)} %bitcast.22), custom_call_target="tpu_custom_call" | custom-call | tf_op jit(solution)/shard_map/k1_body/pallas_call | solution.py:259
  19.0 3.9 %all-to-all-done = s32[32,1,256]{2,1,0:T(1,128)S(1)} async-done(((s32[32,1,256]{2,1,0:T(1,128)}), s32[32,1,256]{2,1,0:T(1,128)S(1)}, u32[]{:S(2)}, u32[]{:S(2)}) %all-to-all-start) | async-done | bytes 32800 | tf_op jit(solution)/shard_map/all_to_all | solution.py:257
  22.9 0.3 k2_body.1
  23.2 12.3 %all_to_all.15 = f32[16,1,2048]{2,1,0:T(1,128)S(1)} all-to-all(f32[16,1,2048]{2,1,0:T(1,128)S(1)} %bitcast.18), channel_id=1, replica_groups=mesh['xh'=2,'y2'=2,'y1'=2,'y0'=2,'xl'=2,'z2'=2,'z1'=2,'z0'=2,'core'=2] {..., dimensions={0} | all-to-all | bytes 262144 | tf_op jit(solution)/shard_map/all_to_all | solution.py:274
  35.5 0.2 k3_body.1
  35.7 19.6 %all_to_all.16 = f32[32,1,1536]{2,1,0:T(1,128)S(1)} all-to-all(f32[32,1,1536]{2,1,0:T(1,128)S(1)} %bitcast.16), channel_id=1, replica_groups=mesh['xh'=2,'y2'=2,'y1'=2,'y0'=2,'xl'=2,'z2'=2,'z1'=2,'z0'=2,'core'=2] {..., dimensions={0} | all-to-all | bytes 393216 | tf_op jit(solution)/shard_map/all_to_all | solution.py:276
  55.3 1.4 %k4_body.1 = (f32[16,128]{1,0:T(8,128)}, f32[8,128]{1,0:T(8,128)}, f32[1,1]{1,0:T(1,128)}) custom-call(f32[384,128]{1,0:T(8,128)S(1)} %bitcast.15, s32[64,128]{1,0:T(8,128)S(1)} %bitcast.20), custom_call_target="tpu_custom_call" | custom-call | tf_op jit(solution)/shard_map/k4_body/pallas_call | solution.py:278
Async XLA Ops:
  2.1 20.8 %all-to-all-start = ((s32[32,1,256]{2,1,0:T(1,128)}), s32[32,1,256]{2,1,0:T(1,128)S(1)}, u32[]{:S(2)}, u32[]{:S(2)}) async-start(s32[32,1,256]{2,1,0:T(1,128)} %bitcast.1), calls=%async_computation | async-start | bytes 65536 | tf_op jit(solution)/shard_map/all_to_all | solution.py:257

commit v10 on v9

--- a/solution.py
+++ b/solution.py
@@ -10,10 +10,10 @@
 
 XH, Y2, Y1, Y0, XL, Z2, Z1, Z0, CORE = AXES = ("xh", "y2", "y1", "y0", "xl", "z2", "z1", "z0", "core")
 COL = (XL, Z2, Z1, Z0, CORE)
-NEAR = (Z2, Z1, Z0, CORE)
+NEAR = (Z0, Z1, Z2, CORE)
 FAR = (XH, Y2, Y1, Y0, XL)
-COL_SENT = (Z2, Z1, Z0, CORE, XL)
-FAR_SENT = (Y0, Y1, XL, XH, Y2)
+COL_SENT = (Z0, Z1, Z2, CORE, XL)
+FAR_SENT = (Y0, Y1, Y2, XL, XH)
 
 NNEAR, NFAR, NCOL, NDEV = 16, 32, 32, 512
 SUP_DEV = 2048
@@ -27,6 +27,11 @@
 
 def iota(shape, dim):
     return lax.broadcasted_iota(I32, shape, dim)
+
+
+def turned(z):
+    low, mid = jnp.bitwise_and(z, 1), jnp.bitwise_and(z, 2)
+    return 4 * low + mid + jnp.right_shift(z, 2)
 
 
 def div30(x):
@@ -67,7 +72,7 @@
     dates = jnp.concatenate([dates_ref[...].reshape(1, 3), jnp.zeros((1, LANES - 3), I32)], 1)
     dates = roll(jnp.broadcast_to(dates, (8, LANES)), DATES_AT)
     for i in range(2):
-        m = 2 * sub + i
+        m = 2 * turned(sub) + i
         own = lookup(words, jnp.where(lane < WORDS, m * WORDS + lane, 0))
         row = jnp.where(lane < WORDS, own, dates)
         for j in (4 * i, 4 * i + 2):
@@ -136,7 +141,7 @@
 def k2_body(got_ref, tab_ref, cand_ref, out_ref, tmp_ref):
     got = got_ref[pl.ds(0, NCOL, stride=2), :]
     src, lane = iota((NCOL, LANES), 0), iota((NCOL, LANES), 1)
-    src = 16 * jnp.bitwise_and(src, 1) + jnp.right_shift(src, 1)
+    src = 16 * jnp.bitwise_and(src, 1) + 2 * turned(jnp.right_shift(src, 2)) + jnp.bitwise_and(jnp.right_shift(src, 1), 1)
     table = jnp.zeros((NCOL, LANES), I32)
     for j in range(3):
         word = jnp.broadcast_to(got[:, DATES_AT + j : DATES_AT + j + 1], (NCOL, LANES))
@@ -168,8 +173,9 @@
     tiles = jnp.transpose(jnp.concatenate(stack, 0))
     tiles = jnp.where(row == 0, bits[0], jnp.where(row == 1, bits[1], tiles))
     for g in range(NNEAR):
-        out_ref[16 * g : 16 * g + 8, :] = tiles[8 * g : 8 * g + 8]
-        out_ref[16 * g + 8 : 16 * g + 16, :] = part
+        at = 16 * (((g >> 1) & 1) * 8 + ((g >> 2) & 1) * 4 + ((g >> 3) & 1) * 2 + (g & 1))
+        out_ref[at : at + 8, :] = tiles[8 * g : 8 * g + 8]
+        out_ref[at + 8 : at + 16, :] = part
 
 
 def k3_body(got_ref, out_ref):
@@ -192,7 +198,7 @@
             for q in range(1, 4):
                 tile = jnp.where(jnp.right_shift(lane, 5) == q, roll(rows[q], 32 * (q - lo)), tile)
             to = 4 * hi + lo
-            at = LAST * sum((to >> b & 1) << p for b, p in ((4, 1), (3, 0), (2, 3), (1, 4), (0, 2)))
+            at = LAST * sum((to >> b & 1) << p for b, p in ((4, 0), (3, 2), (2, 3), (1, 4), (0, 1)))
             out_ref[at : at + 4, :] = jnp.where(jnp.bitwise_and(lane, 15) < 12, tile, 0.0)
             out_ref[at + 4 : at + 12, :] = total
 
@@ -217,7 +223,8 @@
     )
     owned = jnp.concatenate([owned[0:16], owned[16:32]], 1)
     far = lax.axis_index(FAR)
-    words = words_ref[pl.ds(4 * jnp.bitwise_and(far, 15) + 2 * jnp.right_shift(far, 4), 1), :]
+    row = 4 * turned(jnp.bitwise_and(jnp.right_shift(far, 1), 7)) + 2 * jnp.bitwise_and(far, 1)
+    words = words_ref[pl.ds(2 * (row + jnp.right_shift(far, 4)), 1), :]
     place = iota((16, LANES), 0) * LANES + iota((16, LANES), 1)
     slot = div30(place)
     bit = jnp.bitwise_and(jnp.right_shift(lane_gather(words, slot), place - 30 * slot), 1)

time: 57.4 us -> 56.9 us (level)
  no operation moved by 1% of the time
where the time goes in v10:
time: 56.9 us; the launch traced here: 56.6 us
  blocking collectives  31.9 us (56%)
  starting transfers between devices  12.9 us (23%)
  Pallas kernels  7.38 us (13%)
  waiting for transfers between devices  3.77 us (7%)
  between operations  0.66 us (1%)
    all_to_all x1, blocking collectives, per_device(): lax.all_to_all(give2.reshape(NFAR, 1, LAST * LANES), FAR_SENT, 0, 0, tile...  19.5 us
    all_to_all x1, starting transfers between devices, per_device(): lax.all_to_all(give0.reshape(NCOL, 1, 2 * LANES), COL_SENT, 0, 0, tiled=T...  12.9 us
    all_to_all x1, blocking collectives, per_device(): lax.all_to_all(give1.reshape(NNEAR, 1, 16 * LANES), NEAR, 0, 0, tiled=True)  12.4 us
    pallas_call x1, Pallas kernels, per_device(): call(k1_body, [VMEM] * 5, [here((64, NDEV), F32), here((48, 1024), F32)],...  4.01 us
    all_to_all x1, waiting for transfers between devices, per_device(): lax.all_to_all(give0.reshape(NCOL, 1, 2 * LANES), COL_SENT, 0, 0, tiled=T...  3.77 us
    pallas_call x1, Pallas kernels, per_device(): call(k0_body, [VMEM, VMEM, VMEM], here((2 * NCOL, LANES), I32))  1.49 us
    pallas_call x1, Pallas kernels, per_device(): call(k4_body, [VMEM, VMEM], [shape((16, LANES), F32), shape((8, LANES), F...  1.42 us
  transfers between devices with their start and end apart: 1, of which 1 were waited for; matrix products, arithmetic and copies ran while one was open for 0% of the time, Pallas kernels for 7%

profile of v10, /device:TPU:1, one launch (start us, length us, event | category | flops | bytes accessed | tf_op | source)
XLA Modules:
  0.0 56.6 jit_solution(10947990653337295591)
XLA Ops:
  0.6 1.5 %k0_body.1 = s32[64,128]{1,0:T(8,128)} custom-call(s32[1104]{0:T(1024)} %words_ref.1, s32[3]{0:T(128)} %dates_ref.1, s32[8,128]{1,0:T(8,128)} %bitcast.21), custom_call_target="tpu_custom_call" | custom-call | tf_op jit(solution)/shard_map/k0_body/pallas_call | solution.py:261
  2.1 12.9 %all-to-all-start = ((s32[32,1,256]{2,1,0:T(1,128)}), s32[32,1,256]{2,1,0:T(1,128)S(1)}, u32[]{:S(2)}, u32[]{:S(2)}) async-start(s32[32,1,256]{2,1,0:T(1,128)} %bitcast.1), calls=%async_computation | async-start | bytes 65536 | tf_op jit(solution)/shard_map/all_to_all | solution.py:264
  15.0 4.0 %k1_body.1 = (f32[64,512]{1,0:T(8,128)S(1)}, f32[48,1024]{1,0:T(8,128)S(1)}) custom-call(s32[24,128]{1,0:T(8,128)} %bitcast.23, s32[24,128]{1,0:T(8,128)} %bitcast.24, s32[24,128]{1,0:T(8,128)} %bitcast.25, bf16[24,128]{1,0:T(8,128)(2,1)} %bitcast.26, s32[1,1024]{1,0:T(1,128)} %bitcast.22), custom_call_target="tpu_custom_call" | custom-call | tf_op jit(solution)/shard_map/k1_body/pallas_call | solution.py:266
  19.0 3.8 %all-to-all-done = s32[32,1,256]{2,1,0:T(1,128)S(1)} async-done(((s32[32,1,256]{2,1,0:T(1,128)}), s32[32,1,256]{2,1,0:T(1,128)S(1)}, u32[]{:S(2)}, u32[]{:S(2)}) %all-to-all-start) | async-done | bytes 32800 | tf_op jit(solution)/shard_map/all_to_all | solution.py:264
  22.8 0.3 k2_body.1
  23.1 12.4 %all_to_all.15 = f32[16,1,2048]{2,1,0:T(1,128)S(1)} all-to-all(f32[16,1,2048]{2,1,0:T(1,128)S(1)} %bitcast.18), channel_id=1, replica_groups=mesh['xh'=2,'y2'=2,'y1'=2,'y0'=2,'xl'=2,'z2'=2,'z1'=2,'z0'=2,'core'=2] {..., dimensions={0} | all-to-all | bytes 262144 | tf_op jit(solution)/shard_map/all_to_all | solution.py:281
  35.5 0.2 k3_body.1
  35.7 19.5 %all_to_all.16 = f32[32,1,1536]{2,1,0:T(1,128)S(1)} all-to-all(f32[32,1,1536]{2,1,0:T(1,128)S(1)} %bitcast.16), channel_id=1, replica_groups=mesh['xh'=2,'y2'=2,'y1'=2,'y0'=2,'xl'=2,'z2'=2,'z1'=2,'z0'=2,'core'=2] {..., dimensions={0} | all-to-all | bytes 393216 | tf_op jit(solution)/shard_map/all_to_all | solution.py:283
  55.2 1.4 %k4_body.1 = (f32[16,128]{1,0:T(8,128)}, f32[8,128]{1,0:T(8,128)}, f32[1,1]{1,0:T(1,128)}) custom-call(f32[384,128]{1,0:T(8,128)S(1)} %bitcast.15, s32[64,128]{1,0:T(8,128)S(1)} %bitcast.20), custom_call_target="tpu_custom_call" | custom-call | tf_op jit(solution)/shard_map/k4_body/pallas_call | solution.py:285
Async XLA Ops:
  2.1 20.7 %all-to-all-start = ((s32[32,1,256]{2,1,0:T(1,128)}), s32[32,1,256]{2,1,0:T(1,128)S(1)}, u32[]{:S(2)}, u32[]{:S(2)}) async-start(s32[32,1,256]{2,1,0:T(1,128)} %bitcast.1), calls=%async_computation | async-start | bytes 65536 | tf_op jit(solution)/shard_map/all_to_all | solution.py:264

commit v11 on v9

--- a/solution.py
+++ b/solution.py
@@ -13,7 +13,7 @@
 NEAR = (Z2, Z1, Z0, CORE)
 FAR = (XH, Y2, Y1, Y0, XL)
 COL_SENT = (Z2, Z1, Z0, CORE, XL)
-FAR_SENT = (Y0, Y1, XL, XH, Y2)
+FAR_SENT = (Y0, Y1, Y2, XH, XL)
 
 NNEAR, NFAR, NCOL, NDEV = 16, 32, 32, 512
 SUP_DEV = 2048
@@ -192,7 +192,7 @@
             for q in range(1, 4):
                 tile = jnp.where(jnp.right_shift(lane, 5) == q, roll(rows[q], 32 * (q - lo)), tile)
             to = 4 * hi + lo
-            at = LAST * sum((to >> b & 1) << p for b, p in ((4, 1), (3, 0), (2, 3), (1, 4), (0, 2)))
+            at = LAST * sum((to >> b & 1) << p for b, p in ((4, 1), (3, 2), (2, 3), (1, 4), (0, 0)))
             out_ref[at : at + 4, :] = jnp.where(jnp.bitwise_and(lane, 15) < 12, tile, 0.0)
             out_ref[at + 4 : at + 12, :] = total
 

time: 57.4 us -> 58.2 us (1.014)
  blocking collectives: 31.9 us -> 33.1 us
    all_to_all x1, blocking collectives: 19.6 us -> 20.7 us  [per_device(): lax.all_to_all(give2.reshape(NFAR, 1, LAST * LANES), FAR_SENT, 0, 0, tile...]
where the time goes in v11:
time: 58.2 us; the launch traced here: 57.9 us
  blocking collectives  33.1 us (57%)
  starting transfers between devices  12.9 us (22%)
  Pallas kernels  7.38 us (13%)
  waiting for transfers between devices  3.88 us (7%)
  between operations  0.66 us (1%)
    all_to_all x1, blocking collectives, per_device(): lax.all_to_all(give2.reshape(NFAR, 1, LAST * LANES), FAR_SENT, 0, 0, tile...  20.7 us
    all_to_all x1, starting transfers between devices, per_device(): lax.all_to_all(give0.reshape(NCOL, 1, 2 * LANES), COL_SENT, 0, 0, tiled=T...  12.9 us
    all_to_all x1, blocking collectives, per_device(): lax.all_to_all(give1.reshape(NNEAR, 1, 16 * LANES), NEAR, 0, 0, tiled=True)  12.3 us
    pallas_call x1, Pallas kernels, per_device(): call(k1_body, [VMEM] * 5, [here((64, NDEV), F32), here((48, 1024), F32)],...  4.02 us
    all_to_all x1, waiting for transfers between devices, per_device(): lax.all_to_all(give0.reshape(NCOL, 1, 2 * LANES), COL_SENT, 0, 0, tiled=T...  3.88 us
    pallas_call x1, Pallas kernels, per_device(): call(k0_body, [VMEM, VMEM, VMEM], here((2 * NCOL, LANES), I32))  1.49 us
    pallas_call x1, Pallas kernels, per_device(): call(k4_body, [VMEM, VMEM], [shape((16, LANES), F32), shape((8, LANES), F...  1.42 us
  transfers between devices with their start and end apart: 1, of which 1 were waited for; matrix products, arithmetic and copies ran while one was open for 0% of the time, Pallas kernels for 7%

profile of v11, /device:TPU:1, one launch (start us, length us, event | category | flops | bytes accessed | tf_op | source)
XLA Modules:
  0.0 57.9 jit_solution(6718477744646531292)
XLA Ops:
  0.6 1.5 %k0_body.1 = s32[64,128]{1,0:T(8,128)} custom-call(s32[1104]{0:T(1024)} %words_ref.1, s32[3]{0:T(128)} %dates_ref.1, s32[8,128]{1,0:T(8,128)} %bitcast.21), custom_call_target="tpu_custom_call" | custom-call | tf_op jit(solution)/shard_map/k0_body/pallas_call | solution.py:254
  2.1 12.9 %all-to-all-start = ((s32[32,1,256]{2,1,0:T(1,128)}), s32[32,1,256]{2,1,0:T(1,128)S(1)}, u32[]{:S(2)}, u32[]{:S(2)}) async-start(s32[32,1,256]{2,1,0:T(1,128)} %bitcast.1), calls=%async_computation | async-start | bytes 65536 | tf_op jit(solution)/shard_map/all_to_all | solution.py:257
  15.0 4.0 %k1_body.1 = (f32[64,512]{1,0:T(8,128)S(1)}, f32[48,1024]{1,0:T(8,128)S(1)}) custom-call(s32[24,128]{1,0:T(8,128)} %bitcast.23, s32[24,128]{1,0:T(8,128)} %bitcast.24, s32[24,128]{1,0:T(8,128)} %bitcast.25, bf16[24,128]{1,0:T(8,128)(2,1)} %bitcast.26, s32[1,1024]{1,0:T(1,128)} %bitcast.22), custom_call_target="tpu_custom_call" | custom-call | tf_op jit(solution)/shard_map/k1_body/pallas_call | solution.py:259
  19.0 3.9 %all-to-all-done = s32[32,1,256]{2,1,0:T(1,128)S(1)} async-done(((s32[32,1,256]{2,1,0:T(1,128)}), s32[32,1,256]{2,1,0:T(1,128)S(1)}, u32[]{:S(2)}, u32[]{:S(2)}) %all-to-all-start) | async-done | bytes 32800 | tf_op jit(solution)/shard_map/all_to_all | solution.py:257
  22.9 0.3 k2_body.1
  23.2 12.3 %all_to_all.15 = f32[16,1,2048]{2,1,0:T(1,128)S(1)} all-to-all(f32[16,1,2048]{2,1,0:T(1,128)S(1)} %bitcast.18), channel_id=1, replica_groups=mesh['xh'=2,'y2'=2,'y1'=2,'y0'=2,'xl'=2,'z2'=2,'z1'=2,'z0'=2,'core'=2] {..., dimensions={0} | all-to-all | bytes 262144 | tf_op jit(solution)/shard_map/all_to_all | solution.py:274
  35.5 0.2 k3_body.1
  35.7 20.7 %all_to_all.16 = f32[32,1,1536]{2,1,0:T(1,128)S(1)} all-to-all(f32[32,1,1536]{2,1,0:T(1,128)S(1)} %bitcast.16), channel_id=1, replica_groups=mesh['xh'=2,'y2'=2,'y1'=2,'y0'=2,'xl'=2,'z2'=2,'z1'=2,'z0'=2,'core'=2] {..., dimensions={0} | all-to-all | bytes 393216 | tf_op jit(solution)/shard_map/all_to_all | solution.py:276
  56.4 1.4 %k4_body.1 = (f32[16,128]{1,0:T(8,128)}, f32[8,128]{1,0:T(8,128)}, f32[1,1]{1,0:T(1,128)}) custom-call(f32[384,128]{1,0:T(8,128)S(1)} %bitcast.15, s32[64,128]{1,0:T(8,128)S(1)} %bitcast.20), custom_call_target="tpu_custom_call" | custom-call | tf_op jit(solution)/shard_map/k4_body/pallas_call | solution.py:278
Async XLA Ops:
  2.1 20.8 %all-to-all-start = ((s32[32,1,256]{2,1,0:T(1,128)}), s32[32,1,256]{2,1,0:T(1,128)S(1)}, u32[]{:S(2)}, u32[]{:S(2)}) async-start(s32[32,1,256]{2,1,0:T(1,128)} %bitcast.1), calls=%async_computation | async-start | bytes 65536 | tf_op jit(solution)/shard_map/all_to_all | solution.py:257

commit v12 on v11

--- a/solution.py
+++ b/solution.py
@@ -13,7 +13,7 @@
 NEAR = (Z2, Z1, Z0, CORE)
 FAR = (XH, Y2, Y1, Y0, XL)
 COL_SENT = (Z2, Z1, Z0, CORE, XL)
-FAR_SENT = (Y0, Y1, Y2, XH, XL)
+FAR_SENT = (XL, Y0, Y1, Y2, XH)
 
 NNEAR, NFAR, NCOL, NDEV = 16, 32, 32, 512
 SUP_DEV = 2048
@@ -192,7 +192,7 @@
             for q in range(1, 4):
                 tile = jnp.where(jnp.right_shift(lane, 5) == q, roll(rows[q], 32 * (q - lo)), tile)
             to = 4 * hi + lo
-            at = LAST * sum((to >> b & 1) << p for b, p in ((4, 1), (3, 2), (2, 3), (1, 4), (0, 0)))
+            at = LAST * sum((to >> b & 1) << p for b, p in ((4, 0), (3, 1), (2, 2), (1, 3), (0, 4)))
             out_ref[at : at + 4, :] = jnp.where(jnp.bitwise_and(lane, 15) < 12, tile, 0.0)
             out_ref[at + 4 : at + 12, :] = total
 

time: 58.2 us -> 57.8 us (level)
  no operation moved by 1% of the time
where the time goes in v12:
time: 57.8 us; the launch traced here: 57.5 us
  blocking collectives  32.7 us (57%)
  starting transfers between devices  12.9 us (22%)
  Pallas kernels  7.38 us (13%)
  waiting for transfers between devices  3.88 us (7%)
  between operations  0.66 us (1%)
    all_to_all x1, blocking collectives, per_device(): lax.all_to_all(give2.reshape(NFAR, 1, LAST * LANES), FAR_SENT, 0, 0, tile...  20.4 us
    all_to_all x1, starting transfers between devices, per_device(): lax.all_to_all(give0.reshape(NCOL, 1, 2 * LANES), COL_SENT, 0, 0, tiled=T...  12.9 us
    all_to_all x1, blocking collectives, per_device(): lax.all_to_all(give1.reshape(NNEAR, 1, 16 * LANES), NEAR, 0, 0, tiled=True)  12.3 us
    pallas_call x1, Pallas kernels, per_device(): call(k1_body, [VMEM] * 5, [here((64, NDEV), F32), here((48, 1024), F32)],...  4.02 us
    all_to_all x1, waiting for transfers between devices, per_device(): lax.all_to_all(give0.reshape(NCOL, 1, 2 * LANES), COL_SENT, 0, 0, tiled=T...  3.88 us
    pallas_call x1, Pallas kernels, per_device(): call(k0_body, [VMEM, VMEM, VMEM], here((2 * NCOL, LANES), I32))  1.49 us
    pallas_call x1, Pallas kernels, per_device(): call(k4_body, [VMEM, VMEM], [shape((16, LANES), F32), shape((8, LANES), F...  1.42 us
  transfers between devices with their start and end apart: 1, of which 1 were waited for; matrix products, arithmetic and copies ran while one was open for 0% of the time, Pallas kernels for 7%

profile of v12, /device:TPU:1, one launch (start us, length us, event | category | flops | bytes accessed | tf_op | source)
XLA Modules:
  0.0 57.5 jit_solution(6578118712703957355)
XLA Ops:
  0.6 1.5 %k0_body.1 = s32[64,128]{1,0:T(8,128)} custom-call(s32[1104]{0:T(1024)} %words_ref.1, s32[3]{0:T(128)} %dates_ref.1, s32[8,128]{1,0:T(8,128)} %bitcast.21), custom_call_target="tpu_custom_call" | custom-call | tf_op jit(solution)/shard_map/k0_body/pallas_call | solution.py:254
  2.1 12.9 %all-to-all-start = ((s32[32,1,256]{2,1,0:T(1,128)}), s32[32,1,256]{2,1,0:T(1,128)S(1)}, u32[]{:S(2)}, u32[]{:S(2)}) async-start(s32[32,1,256]{2,1,0:T(1,128)} %bitcast.1), calls=%async_computation | async-start | bytes 65536 | tf_op jit(solution)/shard_map/all_to_all | solution.py:257
  15.0 4.0 %k1_body.1 = (f32[64,512]{1,0:T(8,128)S(1)}, f32[48,1024]{1,0:T(8,128)S(1)}) custom-call(s32[24,128]{1,0:T(8,128)} %bitcast.23, s32[24,128]{1,0:T(8,128)} %bitcast.24, s32[24,128]{1,0:T(8,128)} %bitcast.25, bf16[24,128]{1,0:T(8,128)(2,1)} %bitcast.26, s32[1,1024]{1,0:T(1,128)} %bitcast.22), custom_call_target="tpu_custom_call" | custom-call | tf_op jit(solution)/shard_map/k1_body/pallas_call | solution.py:259
  19.0 3.9 %all-to-all-done = s32[32,1,256]{2,1,0:T(1,128)S(1)} async-done(((s32[32,1,256]{2,1,0:T(1,128)}), s32[32,1,256]{2,1,0:T(1,128)S(1)}, u32[]{:S(2)}, u32[]{:S(2)}) %all-to-all-start) | async-done | bytes 32800 | tf_op jit(solution)/shard_map/all_to_all | solution.py:257
  22.9 0.3 k2_body.1
  23.2 12.3 %all_to_all.15 = f32[16,1,2048]{2,1,0:T(1,128)S(1)} all-to-all(f32[16,1,2048]{2,1,0:T(1,128)S(1)} %bitcast.18), channel_id=1, replica_groups=mesh['xh'=2,'y2'=2,'y1'=2,'y0'=2,'xl'=2,'z2'=2,'z1'=2,'z0'=2,'core'=2] {..., dimensions={0} | all-to-all | bytes 262144 | tf_op jit(solution)/shard_map/all_to_all | solution.py:274
  35.5 0.2 k3_body.1
  35.7 20.4 %all_to_all.16 = f32[32,1,1536]{2,1,0:T(1,128)S(1)} all-to-all(f32[32,1,1536]{2,1,0:T(1,128)S(1)} %bitcast.16), channel_id=1, replica_groups=mesh['xh'=2,'y2'=2,'y1'=2,'y0'=2,'xl'=2,'z2'=2,'z1'=2,'z0'=2,'core'=2] {..., dimensions={0} | all-to-all | bytes 393216 | tf_op jit(solution)/shard_map/all_to_all | solution.py:276
  56.1 1.4 %k4_body.1 = (f32[16,128]{1,0:T(8,128)}, f32[8,128]{1,0:T(8,128)}, f32[1,1]{1,0:T(1,128)}) custom-call(f32[384,128]{1,0:T(8,128)S(1)} %bitcast.15, s32[64,128]{1,0:T(8,128)S(1)} %bitcast.20), custom_call_target="tpu_custom_call" | custom-call | tf_op jit(solution)/shard_map/k4_body/pallas_call | solution.py:278
Async XLA Ops:
  2.1 20.8 %all-to-all-start = ((s32[32,1,256]{2,1,0:T(1,128)}), s32[32,1,256]{2,1,0:T(1,128)S(1)}, u32[]{:S(2)}, u32[]{:S(2)}) async-start(s32[32,1,256]{2,1,0:T(1,128)} %bitcast.1), calls=%async_computation | async-start | bytes 65536 | tf_op jit(solution)/shard_map/all_to_all | solution.py:257

commit v13 on v12

--- a/solution.py
+++ b/solution.py
@@ -13,7 +13,7 @@
 NEAR = (Z2, Z1, Z0, CORE)
 FAR = (XH, Y2, Y1, Y0, XL)
 COL_SENT = (Z2, Z1, Z0, CORE, XL)
-FAR_SENT = (XL, Y0, Y1, Y2, XH)
+FAR_SENT = (Y0, Y1, Y2, XL, XH)
 
 NNEAR, NFAR, NCOL, NDEV = 16, 32, 32, 512
 SUP_DEV = 2048
@@ -22,7 +22,7 @@
 CH = 24
 F32, BF16, I32 = jnp.float32, jnp.bfloat16, jnp.int32
 DATES_AT = 104
-LAST = 12
+LAST = 11
 
 
 def iota(shape, dim):
@@ -184,7 +184,7 @@
     for g in range(1, NNEAR):
         total = total + got_ref[16 * g + 8 : 16 * g + 16, :]
     total = total * bits
-    lane = iota((4, LANES), 1)
+    sub, lane = iota((4, LANES), 0), iota((4, LANES), 1)
     for hi in range(8):
         rows = [got_ref[pl.ds(64 * q + hi, 4, stride=16), :] for q in range(4)]
         for lo in range(4):
@@ -192,9 +192,12 @@
             for q in range(1, 4):
                 tile = jnp.where(jnp.right_shift(lane, 5) == q, roll(rows[q], 32 * (q - lo)), tile)
             to = 4 * hi + lo
-            at = LAST * sum((to >> b & 1) << p for b, p in ((4, 0), (3, 1), (2, 2), (1, 3), (0, 4)))
-            out_ref[at : at + 4, :] = jnp.where(jnp.bitwise_and(lane, 15) < 12, tile, 0.0)
-            out_ref[at + 4 : at + 12, :] = total
+            at = LAST * sum((to >> b & 1) << p for b, p in ((4, 0), (3, 2), (2, 3), (1, 4), (0, 1)))
+            fourth = jnp.broadcast_to(tile[3:4], (4, LANES))
+            moved = jnp.where(sub == 0, roll(fourth, 12), jnp.where(sub == 1, roll(fourth, 8), roll(fourth, 4)))
+            tile = jnp.where(jnp.bitwise_and(lane, 15) < 12, tile, moved)
+            out_ref[at : at + 3, :] = tile[0:3]
+            out_ref[at + 3 : at + 11, :] = total
 
 
 def k4_body(got_ref, words_ref, owned_ref, cand_ref, total_ref, hi_ref, lo_ref):
@@ -202,9 +205,18 @@
     first = jnp.bitwise_and(lane, 16) == 0
     high, low = iota((32, LANES), 0), iota((64, LANES), 0)
     high = 2 * jnp.bitwise_and(high, 15) + jnp.right_shift(high, 4)
+    place = jnp.bitwise_and(lane, 15)
+
+    def slots(eight):
+        sent = [got_ref[pl.ds(8 * LAST * eight + u, 8, stride=LAST), :] for u in range(3)]
+        fourth = jnp.zeros((8, LANES), F32)
+        for u in range(3):
+            fourth = jnp.where(jnp.right_shift(place, 2) == u, roll(sent[u], 4 * u - 12), fourth)
+        return [jnp.where(place < 12, x, 0.0) for x in sent] + [fourth]
+
+    tiles = [slots(eight) for eight in range(4)]
     for p in range(8):
-        even = got_ref[pl.ds(16 * LAST * (p // 4) + p % 4, 8, stride=LAST), :]
-        odd = got_ref[pl.ds(16 * LAST * (p // 4) + 8 * LAST + p % 4, 8, stride=LAST), :]
+        even, odd = tiles[2 * (p // 4)][p % 4], tiles[2 * (p // 4) + 1][p % 4]
         off = jnp.where(first, even, roll(odd, 16)).astype(I32)
         rev = jnp.where(first, roll(even, -16), odd)
         off_hi, off_lo = jnp.right_shift(off, 6), jnp.bitwise_and(off, 63)
@@ -222,9 +234,9 @@
     slot = div30(place)
     bit = jnp.bitwise_and(jnp.right_shift(lane_gather(words, slot), place - 30 * slot), 1)
     owned_ref[...] = jnp.where(bit == 1, owned, 0.0)
-    cand = got_ref[4:12, :]
+    cand = got_ref[3:11, :]
     for h in range(1, NFAR):
-        cand = cand + got_ref[LAST * h + 4 : LAST * h + 12, :]
+        cand = cand + got_ref[LAST * h + 3 : LAST * h + 11, :]
     cand_ref[...] = cand
     total_ref[...] = jnp.sum(jnp.sum(cand, axis=0, keepdims=True), axis=1, keepdims=True)
 

time: 57.8 us -> 57.5 us (level)
  blocking collectives: 32.7 us -> 31.6 us
  Pallas kernels: 7.38 us -> 8.25 us
    all_to_all x1, blocking collectives: 20.4 us -> 19.2 us  [per_device(): lax.all_to_all(give2.reshape(NFAR, 1, LAST * LANES), FAR_SENT, 0, 0, tile...]
    pallas_call x1, Pallas kernels: 0.18 us -> 0.99 us  [per_device(): call(k3_body, [VMEM], here((NFAR * LAST, LANES), F32))]
where the time goes in v13:
time: 57.5 us; the launch traced here: 57.2 us
  blocking collectives  31.6 us (55%)
  starting transfers between devices  12.9 us (22%)
  Pallas kernels  8.25 us (14%)
  waiting for transfers between devices  3.88 us (7%)
  between operations  0.66 us (1%)
    all_to_all x1, blocking collectives, per_device(): lax.all_to_all(give2.reshape(NFAR, 1, LAST * LANES), FAR_SENT, 0, 0, tile...  19.2 us
    all_to_all x1, starting transfers between devices, per_device(): lax.all_to_all(give0.reshape(NCOL, 1, 2 * LANES), COL_SENT, 0, 0, tiled=T...  12.9 us
    all_to_all x1, blocking collectives, per_device(): lax.all_to_all(give1.reshape(NNEAR, 1, 16 * LANES), NEAR, 0, 0, tiled=True)  12.3 us
    pallas_call x1, Pallas kernels, per_device(): call(k1_body, [VMEM] * 5, [here((64, NDEV), F32), here((48, 1024), F32)],...  4.02 us
    all_to_all x1, waiting for transfers between devices, per_device(): lax.all_to_all(give0.reshape(NCOL, 1, 2 * LANES), COL_SENT, 0, 0, tiled=T...  3.88 us
    pallas_call x1, Pallas kernels, per_device(): call(k0_body, [VMEM, VMEM, VMEM], here((2 * NCOL, LANES), I32))  1.49 us
    pallas_call x1, Pallas kernels, per_device(): call(k4_body, [VMEM, VMEM], [shape((16, LANES), F32), shape((8, LANES), F...  1.47 us
  transfers between devices with their start and end apart: 1, of which 1 were waited for; matrix products, arithmetic and copies ran while one was open for 0% of the time, Pallas kernels for 7%

profile of v13, /device:TPU:1, one launch (start us, length us, event | category | flops | bytes accessed | tf_op | source)
XLA Modules:
  0.0 57.2 jit_solution(12528788282169519303)
XLA Ops:
  0.6 1.5 %k0_body.1 = s32[64,128]{1,0:T(8,128)} custom-call(s32[1104]{0:T(1024)} %words_ref.1, s32[3]{0:T(128)} %dates_ref.1, s32[8,128]{1,0:T(8,128)} %bitcast.21), custom_call_target="tpu_custom_call" | custom-call | tf_op jit(solution)/shard_map/k0_body/pallas_call | solution.py:266
  2.1 12.9 %all-to-all-start = ((s32[32,1,256]{2,1,0:T(1,128)}), s32[32,1,256]{2,1,0:T(1,128)S(1)}, u32[]{:S(2)}, u32[]{:S(2)}) async-start(s32[32,1,256]{2,1,0:T(1,128)} %bitcast.1), calls=%async_computation | async-start | bytes 65536 | tf_op jit(solution)/shard_map/all_to_all | solution.py:269
  15.0 4.0 %k1_body.1 = (f32[64,512]{1,0:T(8,128)S(1)}, f32[48,1024]{1,0:T(8,128)S(1)}) custom-call(s32[24,128]{1,0:T(8,128)} %bitcast.23, s32[24,128]{1,0:T(8,128)} %bitcast.24, s32[24,128]{1,0:T(8,128)} %bitcast.25, bf16[24,128]{1,0:T(8,128)(2,1)} %bitcast.26, s32[1,1024]{1,0:T(1,128)} %bitcast.22), custom_call_target="tpu_custom_call" | custom-call | tf_op jit(solution)/shard_map/k1_body/pallas_call | solution.py:271
  19.0 3.9 %all-to-all-done = s32[32,1,256]{2,1,0:T(1,128)S(1)} async-done(((s32[32,1,256]{2,1,0:T(1,128)}), s32[32,1,256]{2,1,0:T(1,128)S(1)}, u32[]{:S(2)}, u32[]{:S(2)}) %all-to-all-start) | async-done | bytes 32800 | tf_op jit(solution)/shard_map/all_to_all | solution.py:269
  22.9 0.3 k2_body.1
  23.2 12.3 %all_to_all.15 = f32[16,1,2048]{2,1,0:T(1,128)S(1)} all-to-all(f32[16,1,2048]{2,1,0:T(1,128)S(1)} %bitcast.18), channel_id=1, replica_groups=mesh['xh'=2,'y2'=2,'y1'=2,'y0'=2,'xl'=2,'z2'=2,'z1'=2,'z0'=2,'core'=2] {..., dimensions={0} | all-to-all | bytes 262144 | tf_op jit(solution)/shard_map/all_to_all | solution.py:286
  35.5 1.0 %k3_body.1 = f32[352,128]{1,0:T(8,128)S(1)} custom-call(f32[256,128]{1,0:T(8,128)S(1)} %bitcast.17), custom_call_target="tpu_custom_call" | custom-call | tf_op jit(solution)/shard_map/k3_body/pallas_call | solution.py:287
  36.5 19.2 %all_to_all.16 = f32[32,1,1408]{2,1,0:T(1,128)S(1)} all-to-all(f32[32,1,1408]{2,1,0:T(1,128)S(1)} %bitcast.16), channel_id=1, replica_groups=mesh['xh'=2,'y2'=2,'y1'=2,'y0'=2,'xl'=2,'z2'=2,'z1'=2,'z0'=2,'core'=2] {..., dimensions={0} | all-to-all | bytes 360448 | tf_op jit(solution)/shard_map/all_to_all | solution.py:288
  55.8 1.5 %k4_body.1 = (f32[16,128]{1,0:T(8,128)}, f32[8,128]{1,0:T(8,128)}, f32[1,1]{1,0:T(1,128)}) custom-call(f32[352,128]{1,0:T(8,128)S(1)} %bitcast.15, s32[64,128]{1,0:T(8,128)S(1)} %bitcast.20), custom_call_target="tpu_custom_call" | custom-call | tf_op jit(solution)/shard_map/k4_body/pallas_call | solution.py:290
Async XLA Ops:
  2.1 20.8 %all-to-all-start = ((s32[32,1,256]{2,1,0:T(1,128)}), s32[32,1,256]{2,1,0:T(1,128)S(1)}, u32[]{:S(2)}, u32[]{:S(2)}) async-start(s32[32,1,256]{2,1,0:T(1,128)} %bitcast.1), calls=%async_computation | async-start | bytes 65536 | tf_op jit(solution)/shard_map/all_to_all | solution.py:269

commit v14 on v13

--- a/solution.py
+++ b/solution.py
@@ -172,7 +172,7 @@
         out_ref[16 * g + 8 : 16 * g + 16, :] = part
 
 
-def k3_body(got_ref, out_ref):
+def k3_body(got_ref, out_ref, slot_ref):
     lane = iota((8, LANES), 1)
     source = 16 * jnp.right_shift(jnp.bitwise_and(lane, 31), 2) + 12 + jnp.bitwise_and(lane, 3)
     bits = jnp.zeros((8, LANES), F32)
@@ -184,7 +184,7 @@
     for g in range(1, NNEAR):
         total = total + got_ref[16 * g + 8 : 16 * g + 16, :]
     total = total * bits
-    sub, lane = iota((4, LANES), 0), iota((4, LANES), 1)
+    lane = iota((4, LANES), 1)
     for hi in range(8):
         rows = [got_ref[pl.ds(64 * q + hi, 4, stride=16), :] for q in range(4)]
         for lo in range(4):
@@ -192,12 +192,16 @@
             for q in range(1, 4):
                 tile = jnp.where(jnp.right_shift(lane, 5) == q, roll(rows[q], 32 * (q - lo)), tile)
             to = 4 * hi + lo
-            at = LAST * sum((to >> b & 1) << p for b, p in ((4, 0), (3, 2), (2, 3), (1, 4), (0, 1)))
-            fourth = jnp.broadcast_to(tile[3:4], (4, LANES))
-            moved = jnp.where(sub == 0, roll(fourth, 12), jnp.where(sub == 1, roll(fourth, 8), roll(fourth, 4)))
-            tile = jnp.where(jnp.bitwise_and(lane, 15) < 12, tile, moved)
-            out_ref[at : at + 3, :] = tile[0:3]
-            out_ref[at + 3 : at + 11, :] = total
+            at = sum((to >> b & 1) << p for b, p in ((4, 0), (3, 2), (2, 3), (1, 4), (0, 1)))
+            slot_ref[4 * at : 4 * at + 4, :] = tile
+            out_ref[LAST * at + 3 : LAST * at + 11, :] = total
+    place = jnp.bitwise_and(iota((8, LANES), 1), 15)
+    for eight in range(4):
+        fourth = slot_ref[pl.ds(32 * eight + 3, 8, stride=4), :]
+        for u in range(3):
+            rows = slot_ref[pl.ds(32 * eight + u, 8, stride=4), :]
+            rows = jnp.where(place < 12, rows, roll(fourth, 12 - 4 * u))
+            out_ref[pl.ds(8 * LAST * eight + u, 8, stride=LAST), :] = rows
 
 
 def k4_body(got_ref, words_ref, owned_ref, cand_ref, total_ref, hi_ref, lo_ref):
@@ -284,7 +288,7 @@
         got0, near(tab), near(cand)
     )
     got1 = lax.all_to_all(give1.reshape(NNEAR, 1, 16 * LANES), NEAR, 0, 0, tiled=True)
-    give2 = call(k3_body, [VMEM], here((NFAR * LAST, LANES), F32))(near(got1.reshape(NNEAR * 16, LANES)))
+    give2 = call(k3_body, [VMEM], here((NFAR * LAST, LANES), F32), [pltpu.VMEM((4 * NFAR, LANES), F32)])(near(got1.reshape(NNEAR * 16, LANES)))
     got2 = lax.all_to_all(give2.reshape(NFAR, 1, LAST * LANES), FAR_SENT, 0, 0, tiled=True)
     got2 = got2.reshape(NFAR * LAST, LANES)
     owned, cand, total = call(

time: 57.5 us -> 56.8 us (0.988)
  Pallas kernels: 8.25 us -> 7.51 us
    pallas_call x1, Pallas kernels: 0.99 us -> 0.26 us  [per_device(): call(k3_body, [VMEM], here((NFAR * LAST, LANES), F32), [pltpu.VMEM((4 * N...]
where the time goes in v14:
time: 56.8 us; the launch traced here: 56.5 us
  blocking collectives  31.6 us (56%)
  starting transfers between devices  12.9 us (23%)
  Pallas kernels  7.51 us (13%)
  waiting for transfers between devices  3.88 us (7%)
  between operations  0.66 us (1%)
    all_to_all x1, blocking collectives, per_device(): lax.all_to_all(give2.reshape(NFAR, 1, LAST * LANES), FAR_SENT, 0, 0, tile...  19.2 us
    all_to_all x1, starting transfers between devices, per_device(): lax.all_to_all(give0.reshape(NCOL, 1, 2 * LANES), COL_SENT, 0, 0, tiled=T...  12.9 us
    all_to_all x1, blocking collectives, per_device(): lax.all_to_all(give1.reshape(NNEAR, 1, 16 * LANES), NEAR, 0, 0, tiled=True)  12.3 us
    pallas_call x1, Pallas kernels, per_device(): call(k1_body, [VMEM] * 5, [here((64, NDEV), F32), here((48, 1024), F32)],...  4.02 us
    all_to_all x1, waiting for transfers between devices, per_device(): lax.all_to_all(give0.reshape(NCOL, 1, 2 * LANES), COL_SENT, 0, 0, tiled=T...  3.88 us
    pallas_call x1, Pallas kernels, per_device(): call(k0_body, [VMEM, VMEM, VMEM], here((2 * NCOL, LANES), I32))  1.49 us
    pallas_call x1, Pallas kernels, per_device(): call(k4_body, [VMEM, VMEM], [shape((16, LANES), F32), shape((8, LANES), F...  1.47 us
  transfers between devices with their start and end apart: 1, of which 1 were waited for; matrix products, arithmetic and copies ran while one was open for 0% of the time, Pallas kernels for 7%

profile of v14, /device:TPU:1, one launch (start us, length us, event | category | flops | bytes accessed | tf_op | source)
XLA Modules:
  0.0 56.5 jit_solution(10454169614437188622)
XLA Ops:
  0.6 1.5 %k0_body.1 = s32[64,128]{1,0:T(8,128)} custom-call(s32[1104]{0:T(1024)} %words_ref.1, s32[3]{0:T(128)} %dates_ref.1, s32[8,128]{1,0:T(8,128)} %bitcast.21), custom_call_target="tpu_custom_call" | custom-call | tf_op jit(solution)/shard_map/k0_body/pallas_call | solution.py:270
  2.1 12.9 %all-to-all-start = ((s32[32,1,256]{2,1,0:T(1,128)}), s32[32,1,256]{2,1,0:T(1,128)S(1)}, u32[]{:S(2)}, u32[]{:S(2)}) async-start(s32[32,1,256]{2,1,0:T(1,128)} %bitcast.1), calls=%async_computation | async-start | bytes 65536 | tf_op jit(solution)/shard_map/all_to_all | solution.py:273
  15.0 4.0 %k1_body.1 = (f32[64,512]{1,0:T(8,128)S(1)}, f32[48,1024]{1,0:T(8,128)S(1)}) custom-call(s32[24,128]{1,0:T(8,128)} %bitcast.23, s32[24,128]{1,0:T(8,128)} %bitcast.24, s32[24,128]{1,0:T(8,128)} %bitcast.25, bf16[24,128]{1,0:T(8,128)(2,1)} %bitcast.26, s32[1,1024]{1,0:T(1,128)} %bitcast.22), custom_call_target="tpu_custom_call" | custom-call | tf_op jit(solution)/shard_map/k1_body/pallas_call | solution.py:275
  19.0 3.9 %all-to-all-done = s32[32,1,256]{2,1,0:T(1,128)S(1)} async-done(((s32[32,1,256]{2,1,0:T(1,128)}), s32[32,1,256]{2,1,0:T(1,128)S(1)}, u32[]{:S(2)}, u32[]{:S(2)}) %all-to-all-start) | async-done | bytes 32800 | tf_op jit(solution)/shard_map/all_to_all | solution.py:273
  22.9 0.3 k2_body.1
  23.2 12.3 %all_to_all.15 = f32[16,1,2048]{2,1,0:T(1,128)S(1)} all-to-all(f32[16,1,2048]{2,1,0:T(1,128)S(1)} %bitcast.18), channel_id=1, replica_groups=mesh['xh'=2,'y2'=2,'y1'=2,'y0'=2,'xl'=2,'z2'=2,'z1'=2,'z0'=2,'core'=2] {..., dimensions={0} | all-to-all | bytes 262144 | tf_op jit(solution)/shard_map/all_to_all | solution.py:290
  35.5 0.3 k3_body.1
  35.8 19.2 %all_to_all.16 = f32[32,1,1408]{2,1,0:T(1,128)S(1)} all-to-all(f32[32,1,1408]{2,1,0:T(1,128)S(1)} %bitcast.16), channel_id=1, replica_groups=mesh['xh'=2,'y2'=2,'y1'=2,'y0'=2,'xl'=2,'z2'=2,'z1'=2,'z0'=2,'core'=2] {..., dimensions={0} | all-to-all | bytes 360448 | tf_op jit(solution)/shard_map/all_to_all | solution.py:292
  55.0 1.5 %k4_body.1 = (f32[16,128]{1,0:T(8,128)}, f32[8,128]{1,0:T(8,128)}, f32[1,1]{1,0:T(1,128)}) custom-call(f32[352,128]{1,0:T(8,128)S(1)} %bitcast.15, s32[64,128]{1,0:T(8,128)S(1)} %bitcast.20), custom_call_target="tpu_custom_call" | custom-call | tf_op jit(solution)/shard_map/k4_body/pallas_call | solution.py:294
Async XLA Ops:
  2.1 20.8 %all-to-all-start = ((s32[32,1,256]{2,1,0:T(1,128)}), s32[32,1,256]{2,1,0:T(1,128)S(1)}, u32[]{:S(2)}, u32[]{:S(2)}) async-start(s32[32,1,256]{2,1,0:T(1,128)} %bitcast.1), calls=%async_computation | async-start | bytes 65536 | tf_op jit(solution)/shard_map/all_to_all | solution.py:273
